TPU v7x, 512 devices: a whole 4x8x8 slice. The times are simulated.
512 devices in a mesh: walkers: 128 (over z, y, x_hi), orb: 4 (over x_lo, core).
Axes of the slice: x: 4 (x_hi: 2, x_lo: 2; x = x_hi * 2 + x_lo), y: 8, z: 8, core: 2. Of those that a mesh axis runs over, the one named last changes fastest.
Arguments:
- inverse: float32 [512, 2, 128, 128], P('walkers', None, 'orb'), as said below
- slater: float32 [512, 2, 128, 128], P('walkers', None, 'orb'), may hold values from -1 to 3, as said below
- positions: float32 [512, 3, 256], P('walkers'), may hold values from -2 to 10
- displacements: float32 [512, 3, 256], P('walkers'), may hold values from -0.6 to 0.6
- move_order: int32 [512, 2, 128], P('walkers'), may hold values from 0 to 127, each once within a row
- accepted: int32 [512, 2, 32], P('walkers'), may hold values 0 or 1
- counts: int32 [512], P('walkers'), may hold values from 0 to 2, as said below
- log_amp: float32 [512], P('walkers'), may hold values from -4 to 4
- centers: float32 [3, 1024], replicated, may hold values from 0 to 8
- exponents: float32 [1024], replicated, may hold values from 0.3 to 3
- orbitals: float32 [2, 128, 1024], P(None, 'orb'), may hold values from -0.36 to 0.36
- jastrow: float32 [4], replicated, may hold values from 0.2 to 0.6
Outputs:
- inverse_new: float32 [512, 2, 128, 128], P('walkers', None, 'orb')
- slater_new: float32 [512, 2, 128, 128], P('walkers', None, 'orb')
- positions_new: float32 [512, 3, 256], P('walkers')
- log_amp_new: float32 [512], P('walkers')
- local_energy_new: float32 [512], P('walkers')
- energy_mean: float32 [], replicated
Inputs may be any that keep to these rules, and one draw needn't show every extreme that they name: For every walker and spin, inverse is the inverse of the transpose of slater: the sum over o of slater[w, s, o, e] * inverse[w, s, o, f] is 1 when e = f and 0 otherwise, up to float32 rounding. `slater`: orbital values at the current positions. All counts sum to 512; for every whole m, the counts of the first m * 4 walkers sum to a value within 2 of m * 4, and both ends of that band are reached.
All inputs are finite; a program needn't handle non-finite values. No bound on the sum of `accepted` on one device may be relied on, other than what follows from the above.
Results may differ from a plain program's by a relative error of at most 0.0003.
Values sent between devices are 32-bit elements; how exact they have to be, the bound alone decides.
A program may use at most 64 MiB of HBM per device.

v0:
```python
import functools

import jax
import jax.numpy as jnp
from jax import lax
from jax.sharding import Mesh
from jax.sharding import PartitionSpec as P

NEL = 128
K = 32
MOVES = 32
WALKERS = ("walkers_0", "walkers_1", "walkers_2")


highest = lax.Precision.HIGHEST


def sent_together(arrays, axis, split_dim, concat_dim, along):
    ends, at = ([], 0)
    for a in arrays[:-1]:
        at += a.shape[along]
        ends.append(at)
    both = jnp.concatenate(arrays, axis=along)
    return tuple(
        jnp.split(
            lax.all_to_all(both, axis, split_axis=split_dim, concat_axis=concat_dim, tiled=True),
            ends,
            axis=along,
        )
    )


def by_axis(x, axes):
    return functools.reduce(lax.psum, axes, x)


def nothing_yet(x, identity):
    return jnp.zeros_like(x) + jnp.asarray(identity, x.dtype)


def prefix_by_axis(x, axes, combine, identity):
    before = start = nothing_yet(x, identity)
    total = x
    for axis in reversed(axes):
        devices, place = (lax.axis_size(axis), lax.axis_index(axis))
        pieces = lax.all_gather(total, axis)
        inside, total = (start, start)
        for k in range(devices):
            passed = k < place
            total = combine(total, pieces[k])
            inside = jnp.where(passed, total, inside)
        before = combine(inside, before)
    return before


def with_halo(cells, sides, width):
    for axis, dim in sides:
        count = lax.axis_size(axis)
        ends = count - 1
        head = lax.slice_in_dim(cells, 0, width, axis=dim)
        tail = lax.slice_in_dim(cells, cells.shape[dim] - width, cells.shape[dim], axis=dim)
        cells = jnp.concatenate(
            [
                lax.ppermute(tail, axis, [(i, (i + 1) % count) for i in range(ends)]),
                cells,
                lax.ppermute(head, axis, [((i + 1) % count, i) for i in range(ends)]),
            ],
            axis=dim,
        )
    return cells


def basis_values(points, centers, exponents):
    squares = jnp.zeros((centers.shape[1], points.shape[1]), jnp.float32)
    for component in range(3):
        offset = points[component][None, :] - centers[component][:, None]
        squares = squares + offset * offset
    return jnp.exp(-exponents[:, None] * squares)


def orbital_change(points, steps, centers, exponents, orbitals):
    count = points.shape[1] // 2
    differ = basis_values(points + steps, centers, exponents) - basis_values(
        points, centers, exponents
    )
    spin_up = jnp.dot(
        orbitals[0], differ[:, :count], precision=highest, preferred_element_type=jnp.float32
    )
    spin_down = jnp.dot(
        orbitals[1], differ[:, count:], precision=highest, preferred_element_type=jnp.float32
    )
    return jnp.stack([spin_up, spin_down])


def pair_terms(before, after, jastrow):
    total = before.shape[1]
    old_squares = jnp.zeros((total, total), jnp.float32)
    new_squares = jnp.zeros((total, total), jnp.float32)
    for component in range(3):
        old_offset = before[component][:, None] - before[component][None, :]
        new_offset = after[component][:, None] - after[component][None, :]
        old_squares = old_squares + old_offset * old_offset
        new_squares = new_squares + new_offset * new_offset
    spins = jnp.arange(total) // (total // 2)
    same = spins[:, None] == spins[None, :]
    height = jnp.where(same, jastrow[0], jastrow[1])
    falloff = jnp.where(same, jastrow[2], jastrow[3])
    old_dist = jnp.sqrt(old_squares)
    new_dist = jnp.sqrt(new_squares)
    change = jnp.sum(
        height * (new_dist / (1.0 + falloff * new_dist) - old_dist / (1.0 + falloff * old_dist))
    )
    soft = jnp.sum(1.0 / jnp.sqrt(new_squares + 1.0))
    return (change, soft)


def eliminate(coupling, change):
    size = coupling.shape[-1]
    matrix = jnp.concatenate([coupling, change], axis=-1)
    labels = jnp.arange(size)

    def sweep(index, carry):
        matrix, logsum = carry
        pivot_row = lax.dynamic_slice_in_dim(matrix, index, 1, matrix.ndim - 2)
        pivot = lax.dynamic_slice_in_dim(pivot_row, index, 1, matrix.ndim - 1)
        pivot_row = pivot_row / pivot
        column_now = lax.dynamic_slice_in_dim(matrix, index, 1, matrix.ndim - 1)
        mine = (labels == index)[:, None]
        matrix = jnp.where(mine, pivot_row, matrix - column_now * pivot_row)
        return (matrix, logsum + jnp.log(jnp.abs(pivot[..., 0, 0])))

    start = (matrix, jnp.zeros(coupling.shape[:-2], jnp.float32))
    matrix, logsum = lax.fori_loop(0, size, sweep, start)
    return (matrix[..., size:], logsum)


def run_windows(proposed, current, move_order, accepted):
    labels = jnp.arange(NEL)
    chosen = move_order[:, :, 0:K]
    one_hot = (labels[None, None, :, None] == chosen[:, :, None, :]).astype(jnp.float32)
    proposed_cols = jnp.einsum("wsoe,wsek->wsok", proposed, one_hot, precision=highest)
    local_part = jnp.einsum("wsok,wsoe->wske", proposed_cols, current, precision=highest)
    unit_rows = jnp.swapaxes(one_hot, 2, 3)
    effective = jnp.where(accepted[..., None] == 1, local_part, unit_rows)
    coupling = jnp.einsum("wske,wsel->wskl", effective, one_hot, precision=highest)
    solved, logsum = eliminate(coupling, effective - unit_rows)
    columns = jnp.einsum("wsoe,wsek->wsok", current, one_hot, precision=highest)
    current = current - jnp.einsum("wsok,wske->wsoe", columns, solved, precision=highest)
    return (current, logsum)


def add_counts(earlier, later):
    return earlier + later


def slot_table(first_slot, starts, limits, length):
    slot_ids = first_slot + jnp.arange(length, dtype=jnp.int32)
    inside = (starts[None, :] <= slot_ids[:, None]) & (slot_ids[:, None] < limits[None, :])
    return inside.astype(jnp.float32)


def place_rows(table, matrices, places, scalars):
    return (
        jnp.tensordot(table, matrices, axes=(1, 0), precision=highest),
        jnp.tensordot(table, places, axes=(1, 0), precision=highest),
        jnp.tensordot(table, scalars, axes=(1, 0), precision=highest),
    )


def body(
    inverse,
    slater,
    positions,
    displacements,
    move_order,
    accepted,
    counts,
    log_amp,
    centers,
    exponents,
    orbitals,
    jastrow,
):
    walkers_here = inverse.shape[0]

    def per_walker(pair):
        return orbital_change(pair[0], pair[1], centers, exponents, orbitals)

    orbital_shift = lax.map(per_walker, (positions, displacements))
    labels = jnp.arange(NEL)
    placed = (move_order[:, :, :MOVES, None] == labels[None, None, None, :]).astype(jnp.float32)
    applied = jnp.einsum("wsk,wske->wse", accepted.astype(jnp.float32), placed, precision=highest)
    positions_now = positions + displacements * applied.reshape(walkers_here, 1, 2 * NEL)
    group = lax.axis_size("orb")
    subset = walkers_here // group
    begin = lax.axis_index("orb") * subset
    inverse_whole, slater_whole, shift_whole = sent_together(
        (inverse, slater, orbital_shift), "orb", 0, 2, 1
    )
    order_sub = lax.dynamic_slice_in_dim(move_order, begin, subset, 0)
    flags_sub = lax.dynamic_slice_in_dim(accepted, begin, subset, 0)
    applied_sub = lax.dynamic_slice_in_dim(applied, begin, subset, 0)
    current_whole, logdet_sub = run_windows(
        slater_whole + shift_whole, inverse_whole, order_sub, flags_sub
    )
    slater_done = slater_whole + shift_whole * applied_sub[:, :, None, :]
    logdet_tiled = jnp.broadcast_to(logdet_sub[:, :, None, None], (subset, 2, group, 1))
    current, slater_now, logdet_all = (
        *sent_together((current_whole, slater_done), "orb", 2, 0, 1),
        lax.all_to_all(logdet_tiled, "orb", split_axis=2, concat_axis=0, tiled=True),
    )
    logdet = logdet_all[:, :, 0, 0]

    def walker_pairs(pair):
        return pair_terms(pair[0], pair[1], jastrow)

    jastrow_change, soft_total = lax.map(walker_pairs, (positions, positions_now))
    log_now = log_amp + jnp.sum(logdet, axis=1) + 0.5 * jastrow_change
    energy = (soft_total - 2.0 * NEL) / (2.0 * NEL * (2 * NEL - 1))
    weighted = jnp.sum(counts.astype(jnp.float32) * energy)
    energy_sum = by_axis(weighted, WALKERS)
    energy_mean = energy_sum / (walkers_here * lax.axis_size(WALKERS))
    local_total = jnp.sum(counts)
    offset = prefix_by_axis(local_total, WALKERS, add_counts, jnp.int32(0))
    limits = offset + jnp.cumsum(counts)
    starts = limits - counts
    matrices = jnp.stack([current, slater_now], axis=1)
    scalars = jnp.stack([log_now, energy], axis=1)
    rank_here = lax.axis_index(WALKERS)
    first_slot = rank_here * walkers_here
    below = place_rows(
        slot_table(first_slot - walkers_here, starts, limits, walkers_here),
        matrices,
        positions_now,
        scalars,
    )
    stay = place_rows(
        slot_table(first_slot, starts, limits, walkers_here), matrices, positions_now, scalars
    )
    above = place_rows(
        slot_table(first_slot + walkers_here, starts, limits, walkers_here),
        matrices,
        positions_now,
        scalars,
    )
    out_matrices = jnp.concatenate([below[0], above[0]], axis=0)
    out_positions = jnp.concatenate([below[1], above[1]], axis=0)
    out_scalars = jnp.concatenate([below[2], above[2]], axis=0)
    padded = (
        with_halo(out_matrices, ((WALKERS, 0),), walkers_here),
        with_halo(out_positions, ((WALKERS, 0),), walkers_here),
        with_halo(out_scalars, ((WALKERS, 0),), walkers_here),
    )
    new_matrices = stay[0] + padded[0][:walkers_here] + padded[0][3 * walkers_here :]
    new_positions = stay[1] + padded[1][:walkers_here] + padded[1][3 * walkers_here :]
    new_scalars = stay[2] + padded[2][:walkers_here] + padded[2][3 * walkers_here :]
    return (
        new_matrices[:, 0],
        new_matrices[:, 1],
        new_positions,
        new_scalars[:, 0],
        new_scalars[:, 1],
        energy_mean,
    )


def solution(mesh):
    finer = Mesh(
        mesh.devices.reshape(8, 8, 2, mesh.shape["orb"]),
        ("walkers_0", "walkers_1", "walkers_2", "orb"),
    )
    placed = (
        P(WALKERS, None, "orb", None),
        P(WALKERS, None, "orb", None),
        P(WALKERS, None, None),
        P(WALKERS, None, None),
        P(WALKERS, None, None),
        P(WALKERS, None, None),
        P(WALKERS),
        P(WALKERS),
        P(),
        P(),
        P(None, "orb", None),
        P(),
    )
    return jax.shard_map(
        body,
        mesh=finer,
        in_specs=placed,
        out_specs=(
            P(WALKERS, None, "orb", None),
            P(WALKERS, None, "orb", None),
            P(WALKERS, None, None),
            P(WALKERS),
            P(WALKERS),
            P(),
        ),
        check_vma=False,
    )
```

profile of v0, /device:TPU:11, one launch (start us, length us, event | category | flops | bytes accessed | tf_op | source)
XLA Modules:
  0.0 234.9 jit_solution(9671037526781243335)
XLA Ops:
  1.4 23.7 %while.45 = (s32[]{:T(128)}, f32[4,2,32,128]{3,2,1,0:T(8,128)S(1)}, f32[1024,1]{0,1:T(1,128)S(1)}, f32[4,3,256]{2,0,1:T(4,128)}, f32[4,3,256]{2,0,1:T(4,128)}, /...) while((s32[]{:T(128)}, f32[4,2,32,128]{3,2,1,0:T(8,128)S(1)}, ...), condition=%wide.region_3.4_spmd, body=%wide.region_2.3_spmd.sunk | while | flops 105652992 | bytes 2526361 | solution.py:189
  25.9 4.2 %all-to-all-start = ((f32[4,6,32,128]{3,2,1,0:T(8,128)}), f32[4,6,32,128]{3,2,1,0:T(8,128)S(1)}, u32[]{:S(2)}, u32[]{:S(2)}) async-start(f32[4,6,32,128]{3,2,1,0:T(8,128)} %pad_maximum_fusion), calls=%async_computation | async-start | bytes 786432 | tf_op jit(solution)/shard_map/all_to_all | solution.py:26
  33.5 4.6 %all-reduce = s32[2]{0:T(128)S(1)} all-reduce(s32[2]{0:T(128)S(1)} %dynamic-update-slice), channel_id=1, replica_groups=mesh['walkers_0'=8,'walkers_1'=8,'walkers_2'=2,'orb'=4] {'walkers_2'}, use_global_device_ids=true, to_apply=%add | all-reduce | flops 2 | bytes 16
  42.0 10.3 %all-reduce.1 = s32[8]{0:T(128)S(1)} all-reduce(s32[8]{0:T(128)S(1)} %dynamic-update-slice.1), channel_id=1, replica_groups=mesh['walkers_0'=8,'walkers_1'=8,'walkers_2'=2,'orb'=4] {'walkers_1'}, use_global_device_ids=true, to_apply=%add.1 | all-reduce | flops 8 | bytes 64
  60.2 15.9 %all-reduce.2 = s32[8]{0:T(128)S(1)} all-reduce(s32[8]{0:T(128)S(1)} %dynamic-update-slice.2), channel_id=1, replica_groups=mesh['walkers_0'=8,'walkers_1'=8,'walkers_2'=2,'orb'=4] {'walkers_0'}, use_global_device_ids=true, to_apply=%add.2 | all-reduce | flops 8 | bytes 64
  85.3 4.1 %collective-permute-start.2 = (f32[4,3,256]{2,0,1:T(4,128)S(1)}, f32[4,3,256]{2,0,1:T(4,128)S(1)}, u32[]{:S(2)}, u32[]{:S(2)}) collective-permute-start(f32[4,3,256]{2,0,1:T(4,128)S(1)} %fusion.43), channel_id=1, source_target_pairs={{0,4},{4,8},{8,12},{12,16},{16,20},{20,24},{24,28},{28,32},{32,36}... | collective-permute-start | bytes 36872 | tf_op jit(solution)/shard_map/ppermute | solution.py:64
  89.5 3.6 %collective-permute-start.3 = (f32[4,3,256]{2,0,1:T(4,128)S(1)}, f32[4,3,256]{2,0,1:T(4,128)S(1)}, u32[]{:S(2)}, u32[]{:S(2)}) collective-permute-start(f32[4,3,256]{2,0,1:T(4,128)S(1)} %fusion.41), channel_id=1, source_target_pairs={{4,0},{8,4},{12,8},{16,12},{20,16},{24,20},{28,24},{32,28},{36,32}... | collective-permute-start | bytes 36872 | tf_op jit(solution)/shard_map/ppermute | solution.py:66
  93.2 26.5 %while.46 = (s32[]{:T(128)}, f32[4]{0:T(128)S(1)}, f32[4]{0:T(128)S(1)}, f32[4]{0:T(128)S(1)}, f32[4,3,256]{2,1,0:T(4,128)S(1)}, /*index=5*/f32[4,3,256]{2,0,1:T(4,128)}, s32[]{:T(128)}, s32[]{:T(128)}, s32[]{}, s32[]{}) while((s32[]{:T(128)}, f32[4]{0:T(128)S(1)}, f32[4]{0:T(128)S(1)}, f32[4]{0:T(128)S(1)}, f32[4,3,256]{2,1,0:T(4,128)S(1)}, ...), condition=%wide.region_10.11_spmd, body=%wide.region_7.10_spmd.sunk | while | flops 1968130 | bytes 20709 | solution.py:217
  94.5 3.8 %rsqrt_reduce_fusion.2 = (f32[]{:T(128)}, f32[]{:T(128)}) fusion(f32[256]{0:T(256)S(1)} %bitcast.265, f32[256]{0:T(256)S(1)} %bitcast.264, f32[256]{0:T(256)S(1)} %bitcast.263, f32[256]{0:T(256)S(1)} %bitcast.268, f32[256]{0:T(256)S(1)} %bitcast.267, f32[256]{0:T(256)S(1)} %bitcast.266, f32[]{:T(128)} %bitcast.233, f32[]{:T(128)} %bitcast.234, ...), kind=kLoop, calls=%fused_computation.26.clone.1 | loop fusion | flops 1966078 | bytes 7192 | tf_op jit(solution)/shard_map/while/body/eval_jaxpr/reduce_sum | solution.py:113
  101.2 3.8 %rsqrt_reduce_fusion.2 = (f32[]{:T(128)}, f32[]{:T(128)}) fusion(f32[256]{0:T(256)S(1)} %bitcast.265, f32[256]{0:T(256)S(1)} %bitcast.264, f32[256]{0:T(256)S(1)} %bitcast.263, f32[256]{0:T(256)S(1)} %bitcast.268, f32[256]{0:T(256)S(1)} %bitcast.267, f32[256]{0:T(256)S(1)} %bitcast.266, f32[]{:T(128)} %bitcast.233, f32[]{:T(128)} %bitcast.234, ...), kind=kLoop, calls=%fused_computation.26.clone.1 | loop fusion | flops 1966078 | bytes 7192 | tf_op jit(solution)/shard_map/while/body/eval_jaxpr/reduce_sum | solution.py:113
  107.8 3.8 %rsqrt_reduce_fusion.2 = (f32[]{:T(128)}, f32[]{:T(128)}) fusion(f32[256]{0:T(256)S(1)} %bitcast.265, f32[256]{0:T(256)S(1)} %bitcast.264, f32[256]{0:T(256)S(1)} %bitcast.263, f32[256]{0:T(256)S(1)} %bitcast.268, f32[256]{0:T(256)S(1)} %bitcast.267, f32[256]{0:T(256)S(1)} %bitcast.266, f32[]{:T(128)} %bitcast.233, f32[]{:T(128)} %bitcast.234, ...), kind=kLoop, calls=%fused_computation.26.clone.1 | loop fusion | flops 1966078 | bytes 7192 | tf_op jit(solution)/shard_map/while/body/eval_jaxpr/reduce_sum | solution.py:113
  114.4 3.8 %rsqrt_reduce_fusion.2 = (f32[]{:T(128)}, f32[]{:T(128)}) fusion(f32[256]{0:T(256)S(1)} %bitcast.265, f32[256]{0:T(256)S(1)} %bitcast.264, f32[256]{0:T(256)S(1)} %bitcast.263, f32[256]{0:T(256)S(1)} %bitcast.268, f32[256]{0:T(256)S(1)} %bitcast.267, f32[256]{0:T(256)S(1)} %bitcast.266, f32[]{:T(128)} %bitcast.233, f32[]{:T(128)} %bitcast.234, ...), kind=kLoop, calls=%fused_computation.26.clone.1 | loop fusion | flops 1966078 | bytes 7192 | tf_op jit(solution)/shard_map/while/body/eval_jaxpr/reduce_sum | solution.py:113
  120.3 12.5 %psum.21 = f32[]{:T(128)} all-reduce(f32[]{:T(128)} %get-tuple-element.412), channel_id=1, replica_groups=mesh['walkers_0'=8,'walkers_1'=8,'walkers_2'=2,'orb'=4] {'walkers_0'}, use_global_device_ids=true, to_apply=%region_12.13 | all-reduce | flops 1 | bytes 8 | tf_op jit(solution)/shard_map/psum | solution.py:34
  132.8 14.4 %psum.22 = f32[]{:T(128)} all-reduce(f32[]{:T(128)} %psum.21), channel_id=1, replica_groups=mesh['walkers_0'=8,'walkers_1'=8,'walkers_2'=2,'orb'=4] {'walkers_1'}, use_global_device_ids=true, to_apply=%region_13.14 | all-reduce | flops 1 | bytes 8 | tf_op jit(solution)/shard_map/psum | solution.py:34
  147.3 5.9 %psum.23 = f32[]{:T(128)} all-reduce(f32[]{:T(128)} %psum.22), channel_id=1, replica_groups=mesh['walkers_0'=8,'walkers_1'=8,'walkers_2'=2,'orb'=4] {'walkers_2'}, use_global_device_ids=true, to_apply=%region_14.15 | all-reduce | flops 1 | bytes 8 | tf_op jit(solution)/shard_map/psum | solution.py:34
  156.5 21.1 %while.47 = (s32[]{:T(128)}, f32[1,2,32,160]{1,3,2,0:T(8,128)S(1)}, f32[1,2]{1,0:T(1,128)S(1)}, s32[]{:T(128)}, s32[]{:T(128)}, /*index=5*/s32[]{:T(128)}, s32[]{:T(128)}) while((s32[]{:T(128)}, f32[1,2,32,160]{1,3,2,0:T(8,128)S(1)}, f32[1,2]{1,0:T(1,128)S(1)}, s32[]{:T(128)}, s32[]{:T(128)}, /*index=5*/s32[]{:T(128)}, ...), condition=%wide.region_5.6_spmd.clone, body=%wide.region_4.5_spmd.clone.sunk | while | flops 31083 | bytes 86787 | solution.py:133
  178.2 19.4 %all-to-all-start.2 = ((f32[1,2,4,1]{1,3,0,2:T(1,128)}), f32[1,2,4,1]{1,3,0,2:T(1,128)S(1)}, u32[]{:S(2)}, u32[]{:S(2)}) async-start(f32[1,2,4,1]{1,3,0,2:T(1,128)} %broadcast_in_dim.134), calls=%async_computation.2 | async-start | bytes 4096 | tf_op jit(solution)/shard_map/all_to_all | solution.py:210
  200.2 4.5 %all-to-all-start.1 = ((f32[1,4,128,128]{3,1,0,2:T(4,128)}), f32[1,4,128,128]{3,1,0,2:T(4,128)S(1)}, u32[]{:S(2)}, u32[]{:S(2)}) async-start(f32[1,4,128,128]{3,1,0,2:T(4,128)} %copy.64), calls=%async_computation.1 | async-start | bytes 524288 | tf_op jit(solution)/shard_map/all_to_all | solution.py:26
  205.0 1.9 collective-permute-start.4
  207.1 5.8 %collective-permute-start.5 = (f32[4,2]{0,1:T(2,128)S(1)}, f32[4,2]{0,1:T(2,128)S(1)}, u32[]{:S(2)}, u32[]{:S(2)}) collective-permute-start(f32[4,2]{0,1:T(2,128)S(1)} %fusion.64), channel_id=1, source_target_pairs={{4,0},{8,4},{12,8},{16,12},{20,16},{24,20},{28,24},{32,28},{36,32}... | collective-permute-start | bytes 104 | tf_op jit(solution)/shard_map/ppermute | solution.py:66
  213.9 1.9 collective-permute-start
  215.8 5.8 %collective-permute-start.1 = (f32[4,2,2,32,128]{4,0,3,2,1:T(4,128)S(1)}, f32[4,2,2,32,128]{4,0,3,2,1:T(4,128)S(1)}, u32[]{:S(2)}, u32[]{:S(2)}) collective-permute-start(f32[4,2,2,32,128]{4,0,3,2,1:T(4,128)S(1)} %fusion.34), channel_id=1, source_target_pairs={{4,0},{8,4},{12,8},{16,12},{20,16},{24,20},{28,24},{32,28},{36,32}... | collective-permute-start | bytes 786440 | tf_op jit(solution)/shard_map/ppermute | solution.py:66
  222.2 4.0 %collective-permute-done = f32[4,2,2,32,128]{4,0,3,2,1:T(4,128)S(1)} collective-permute-done((f32[4,2,2,32,128]{4,0,3,2,1:T(4,128)S(1)}, f32[4,2,2,32,128]{4,0,3,2,1:T(4,128)S(1)}, u32[]{:S(2)}, u32[]{:S(2)}) %collective-permute-start) | collective-permute-done | bytes 262176 | tf_op jit(solution)/shard_map/ppermute | solution.py:64
  226.2 5.8 %collective-permute-done.1 = f32[4,2,2,32,128]{4,0,3,2,1:T(4,128)S(1)} collective-permute-done((f32[4,2,2,32,128]{4,0,3,2,1:T(4,128)S(1)}, f32[4,2,2,32,128]{4,0,3,2,1:T(4,128)S(1)}, u32[]{:S(2)}, u32[]{:S(2)}) %collective-permute-start.1) | collective-permute-done | bytes 262176 | tf_op jit(solution)/shard_map/ppermute | solution.py:66
  (333 shorter events, 76.8 us)
Async XLA Ops:
  1.3 23.8 %copy-start.1 = (f32[4,2,32,128]{3,2,1,0:T(8,128)S(1)}, f32[4,2,32,128]{3,2,1,0:T(8,128)}, u32[]{:S(2)}) copy-start(f32[4,2,32,128]{3,2,1,0:T(8,128)} %param.19) | copy-start | bytes 393220
  1.3 23.8 %copy-start.2 = (f32[4,2,32,128]{3,2,1,0:T(8,128)S(1)}, f32[4,2,32,128]{3,2,1,0:T(8,128)}, u32[]{:S(2)}) copy-start(f32[4,2,32,128]{3,2,1,0:T(8,128)} %param.18) | copy-start | bytes 393220
  1.3 30.1 %copy-start.4 = (s32[4]{0:T(128)S(1)}, s32[4]{0:T(128)}, u32[]{:S(2)}) copy-start(s32[4]{0:T(128)} %param.24) | copy-start | bytes 52
  1.3 75.5 %copy-start.3 = (s32[4,2,32]{2,1,0:T(2,128)S(1)}, s32[4,2,32]{2,1,0:T(2,128)}, u32[]{:S(2)}) copy-start(s32[4,2,32]{2,1,0:T(2,128)} %param.23) | copy-start | bytes 3076
  1.3 75.5 %copy-start.6 = (s32[4,2,128]{2,1,0:T(2,128)S(1)}, s32[4,2,128]{2,1,0:T(2,128)}, u32[]{:S(2)}) copy-start(s32[4,2,128]{2,1,0:T(2,128)} %param.22) | copy-start | bytes 12292
  1.4 91.8 %copy-start = (f32[4]{0:T(128)S(1)}, f32[4]{0:T(128)}, u32[]{:S(2)}) copy-start(f32[4]{0:T(128)} %param.29) | copy-start | bytes 52
  25.9 128.7 %all-to-all-start = ((f32[4,6,32,128]{3,2,1,0:T(8,128)}), f32[4,6,32,128]{3,2,1,0:T(8,128)S(1)}, u32[]{:S(2)}, u32[]{:S(2)}) async-start(f32[4,6,32,128]{3,2,1,0:T(8,128)} %pad_maximum_fusion), calls=%async_computation | async-start | bytes 786432 | tf_op jit(solution)/shard_map/all_to_all | solution.py:26
  85.3 68.5 %collective-permute-start.2 = (f32[4,3,256]{2,0,1:T(4,128)S(1)}, f32[4,3,256]{2,0,1:T(4,128)S(1)}, u32[]{:S(2)}, u32[]{:S(2)}) collective-permute-start(f32[4,3,256]{2,0,1:T(4,128)S(1)} %fusion.43), channel_id=1, source_target_pairs={{0,4},{4,8},{8,12},{12,16},{16,20},{20,24},{24,28},{28,32},{32,36}... | collective-permute-start | bytes 36872 | tf_op jit(solution)/shard_map/ppermute | solution.py:64
  89.5 64.3 %collective-permute-start.3 = (f32[4,3,256]{2,0,1:T(4,128)S(1)}, f32[4,3,256]{2,0,1:T(4,128)S(1)}, u32[]{:S(2)}, u32[]{:S(2)}) collective-permute-start(f32[4,3,256]{2,0,1:T(4,128)S(1)} %fusion.41), channel_id=1, source_target_pairs={{4,0},{8,4},{12,8},{16,12},{20,16},{24,20},{28,24},{32,28},{36,32}... | collective-permute-start | bytes 36872 | tf_op jit(solution)/shard_map/ppermute | solution.py:66
  177.6 27.2 %copy-start.5 = (f32[4]{0:T(128)S(1)}, f32[4]{0:T(128)}, u32[]{:S(2)}) copy-start(f32[4]{0:T(128)} %param.25) | copy-start | bytes 52
  178.2 22.0 %all-to-all-start.2 = ((f32[1,2,4,1]{1,3,0,2:T(1,128)}), f32[1,2,4,1]{1,3,0,2:T(1,128)S(1)}, u32[]{:S(2)}, u32[]{:S(2)}) async-start(f32[1,2,4,1]{1,3,0,2:T(1,128)} %broadcast_in_dim.134), calls=%async_computation.2 | async-start | bytes 4096 | tf_op jit(solution)/shard_map/all_to_all | solution.py:210
  200.2 12.6 %all-to-all-start.1 = ((f32[1,4,128,128]{3,1,0,2:T(4,128)}), f32[1,4,128,128]{3,1,0,2:T(4,128)S(1)}, u32[]{:S(2)}, u32[]{:S(2)}) async-start(f32[1,4,128,128]{3,1,0,2:T(4,128)} %copy.64), calls=%async_computation.1 | async-start | bytes 524288 | tf_op jit(solution)/shard_map/all_to_all | solution.py:26
  205.0 16.5 %collective-permute-start.4 = (f32[4,2]{0,1:T(2,128)S(1)}, f32[4,2]{0,1:T(2,128)S(1)}, u32[]{:S(2)}, u32[]{:S(2)}) collective-permute-start(f32[4,2]{0,1:T(2,128)S(1)} %fusion.63), channel_id=1, source_target_pairs={{0,4},{4,8},{8,12},{12,16},{16,20},{20,24},{24,28},{28,32},{32,36}... | collective-permute-start | bytes 104 | tf_op jit(solution)/shard_map/ppermute | solution.py:64
  207.1 14.5 %collective-permute-start.5 = (f32[4,2]{0,1:T(2,128)S(1)}, f32[4,2]{0,1:T(2,128)S(1)}, u32[]{:S(2)}, u32[]{:S(2)}) collective-permute-start(f32[4,2]{0,1:T(2,128)S(1)} %fusion.64), channel_id=1, source_target_pairs={{4,0},{8,4},{12,8},{16,12},{20,16},{24,20},{28,24},{32,28},{36,32}... | collective-permute-start | bytes 104 | tf_op jit(solution)/shard_map/ppermute | solution.py:66
  213.9 12.4 %collective-permute-start = (f32[4,2,2,32,128]{4,0,3,2,1:T(4,128)S(1)}, f32[4,2,2,32,128]{4,0,3,2,1:T(4,128)S(1)}, u32[]{:S(2)}, u32[]{:S(2)}) collective-permute-start(f32[4,2,2,32,128]{4,0,3,2,1:T(4,128)S(1)} %fusion.35), channel_id=1, source_target_pairs={{0,4},{4,8},{8,12},{12,16},{16,20},{20,24},{24,28},{28,32},{32,36}... | collective-permute-start | bytes 786440 | tf_op jit(solution)/shard_map/ppermute | solution.py:64
  215.8 16.2 %collective-permute-start.1 = (f32[4,2,2,32,128]{4,0,3,2,1:T(4,128)S(1)}, f32[4,2,2,32,128]{4,0,3,2,1:T(4,128)S(1)}, u32[]{:S(2)}, u32[]{:S(2)}) collective-permute-start(f32[4,2,2,32,128]{4,0,3,2,1:T(4,128)S(1)} %fusion.34), channel_id=1, source_target_pairs={{4,0},{8,4},{12,8},{16,12},{20,16},{24,20},{28,24},{32,28},{36,32}... | collective-permute-start | bytes 786440 | tf_op jit(solution)/shard_map/ppermute | solution.py:66
where the time goes:
time: 238 us; the launch traced here: 235 us
  blocking collectives  63.7 us (27%)
  starting transfers between devices  51.3 us (22%)
  other arithmetic  43.6 us (18%)
  local copies, waits for them, and re-layouts  33.4 us (14%)
  between operations  16.3 us (7%)
  matrix products  14.7 us (6%)
  waiting for transfers between devices  9.78 us (4%)
    psum x3, blocking collectives, by_axis(): return functools.reduce(lax.psum, axes, x)  32.8 us
    unnamed x3, blocking collectives  30.8 us
    all_to_all x1, starting transfers between devices, body(): lax.all_to_all(logdet_tiled, 'orb', split_axis=2, concat_axis=0, tiled=True)  19.4 us
    select_n x32, other arithmetic, sweep(): matrix = jnp.where(mine, pivot_row, matrix - column_now * pivot_row)  16.4 us
    ppermute x3, starting transfers between devices, with_halo(): lax.ppermute(head, axis, [((i + 1) % count, i) for i in range(ends)])  15.1 us
    reduce_sum x4, other arithmetic, pair_terms(): soft = jnp.sum(1.0 / jnp.sqrt(new_squares + 1.0))  15 us
    unnamed x27, local copies, waits for them, and re-layouts  8.99 us
    all_to_all x2, starting transfers between devices, sent_together(): lax.all_to_all(both, axis, split_axis=split_dim, concat_axis=concat_dim,...  8.78 us
  transfers between devices with their start and end apart: 9, of which 2 were waited for; matrix products, arithmetic and copies ran while one was open for 18% of the time, Pallas kernels for 0%

commit v1 on v0

v1 whole, which is shorter than its diff:
```python
import math

import jax
import jax.numpy as jnp
from jax import lax
from jax.experimental import pallas as pl
from jax.experimental.pallas import tpu as pltpu
from jax.sharding import PartitionSpec as P

NEL = 128
K = 32
WD = 4
F32 = jnp.float32
BF16 = jnp.bfloat16
MESH = pl.DeviceIdType.MESH
LOG2E = math.log2(math.e)


def split(x):
    high = x.astype(BF16)
    return high, (x - high.astype(F32)).astype(BF16)


def product(a, b, dims):
    return lax.dot_general(a, b, (dims, ((), ())), preferred_element_type=F32)


NN = ((1,), (0,))
NT = ((1,), (1,))
TN = ((0,), (0,))


def product3(a, b, dims=NN):
    ah, al = a
    bh, bl = b
    return product(ah, bh, dims) + product(ah, bl, dims) + product(al, bh, dims)


def iota(shape, dim):
    return lax.broadcasted_iota(jnp.int32, shape, dim)


def flag(cond):
    return jnp.full((8, 128), cond.astype(jnp.int32), jnp.int32) == 1


def splat(x):
    return jnp.broadcast_to(x, (8, 128))


def pick(mask, new, old):
    rows = new.shape[0]
    new3, old3 = new.reshape(rows // 8, 8, 128), old.reshape(rows // 8, 8, 128)
    return jnp.where(mask[None], new3, old3).reshape(rows, 128)


def kernel(
    planes,
    plane,
    counts,
    jastrow,
    log_amp,
    inv_hbm,
    sla_hbm,
    pos_hbm,
    dis_hbm,
    mo_hbm,
    acc_hbm,
    cen_hbm,
    ex_hbm,
    orb_hbm,
    out_inv,
    out_sla,
    out_pos,
    out_log,
    out_en,
    out_mean,
    inv,
    sla,
    pos,
    dis,
    mo,
    acc,
    cen,
    ex,
    orb,
    dhi,
    dlo,
    oh,
    oha,
    ac,
    misc,
    here,
    logt,
    snd_a,
    part,
    rcv_a,
    rcv_b,
    solv,
    sla_r,
    sla_l,
    rs_r,
    rs_l,
    inv_r,
    inv_l,
    ri_r,
    ri_l,
    row_a,
    row_b,
    tab_a,
    tab_b,
    in_sem,
    send_x,
    recv_x,
    send_a,
    recv_a,
    send_b,
    recv_b,
):
    me = lax.axis_index("walkers")
    ob = lax.axis_index("orb")
    walkers = planes * plane
    core = ob % 2
    partner = (ob // 2) * 2 + (1 - core)
    across = (1 - ob // 2) * 2 + core
    right = (me + 1) % walkers
    left = (me + walkers - 1) % walkers
    z, r = me // plane, me % plane

    def at(w, o):
        return {"walkers": w, "orb": o}

    barrier = pltpu.get_barrier_semaphore()

    def greet(w, o):
        pl.semaphore_signal(barrier, inc=1, device_id=at(w, o), device_id_type=MESH)

    greet(me, partner)
    greet(me, across)
    greet(right, ob)
    greet(left, ob)

    @pl.loop(1, plane)
    def _(t):
        greet(z * plane + (r + t) % plane, ob)

    @pl.loop(1, planes)
    def _(t):
        greet(((z + t) % planes) * plane + r, ob)

    loads = [
        pltpu.make_async_copy(src, dst, in_sem.at[n])
        for n, (src, dst) in enumerate(
            (
                (mo_hbm, mo),
                (acc_hbm, acc),
                (pos_hbm, pos),
                (dis_hbm, dis),
                (cen_hbm, cen),
                (ex_hbm, ex),
                (orb_hbm, orb),
                (inv_hbm, inv),
                (sla_hbm, sla),
            )
        )
    ]
    for load in loads:
        load.start()
    for load in loads[:6]:
        load.wait()

    for w in range(WD):
        for c in range(3):
            for s in range(2):
                cols = slice(s * NEL, (s + 1) * NEL)
                n = 2 * c + s
                here[w, n : n + 1, :] = pos[c, w : w + 1, cols]
                here[w, n + 8 : n + 9, :] = dis[c, w : w + 1, cols]

    lane = iota((K, 128), 1)
    diag = lane == iota((K, 128), 0)

    @pl.loop(0, 2 * WD)
    def _(b):
        w, s = b // 2, b % 2
        order = mo[pl.ds(b, 1), :].astype(F32)
        taken = acc[pl.ds(b, 1), :].astype(F32)
        ek = jnp.sum(jnp.where(diag, order, 0.0), axis=1, keepdims=True)
        ak = jnp.sum(
            jnp.where(diag[:, :K], taken, 0.0), axis=1, keepdims=True
        )
        one = jnp.where(lane.astype(F32) == ek, 1.0, 0.0)
        took = one * ak
        rows = pl.ds(pl.multiple_of(b * K, K), K)
        oh[rows, :] = one.astype(BF16)
        oha[rows, :] = took.astype(BF16)
        ac[rows, :] = jnp.broadcast_to(ak, (K, 128))
        applied = jnp.sum(took, axis=0, keepdims=True)
        old, new = [], []
        for c in range(3):
            p = here[w, pl.ds(2 * c + s, 1), :]
            d = here[w, pl.ds(2 * c + s + 8, 1), :]
            old.append(jnp.sum(one * p, axis=1, keepdims=True))
            new.append(jnp.sum(one * (p + d), axis=1, keepdims=True))
            misc[w, pl.ds(2 * c + s, 1), :] = p + d * applied
        old = [jnp.broadcast_to(v, (K, 128)) for v in old]
        new = [jnp.broadcast_to(v, (K, 128)) for v in new]
        to = pl.ds(pl.multiple_of(w * K, K), K)
        for n in range(8):
            span = slice(n * 128, (n + 1) * 128)
            rate = ex[n : n + 1, :] * (-LOG2E)
            far = jnp.zeros((K, 128), F32)
            near = jnp.zeros((K, 128), F32)
            for c in range(3):
                center = cen[c : c + 1, span]
                a, e = old[c] - center, new[c] - center
                far = far + a * a
                near = near + e * e
            differ = jnp.exp2(rate * near) - jnp.exp2(rate * far)
            high, low = split(differ)
            dhi[s, to, span] = high
            dlo[s, to, span] = low

    loads[6].wait()
    shift = []
    for s in range(2):
        high, low = split(orb[s])
        high4 = jnp.concatenate([high] * 4, axis=0)
        low4 = jnp.concatenate([low] * 4, axis=0)
        a = dhi[s]
        shift.append(product(a, high4, NT) + product(a, low4, NT) + product(dlo[s], high4, NT))

    seg = iota((K, 128), 1) // K

    def block_rows(parts):
        return jnp.concatenate(
            [jnp.where(seg == n, x, 0.0) for n, x in enumerate(parts)], axis=0
        )

    shift_blocks = []
    for g in range(2):
        shift_blocks.append(
            split(
                block_rows(
                    [
                        shift[b % 2][(2 * g + b // 2) * K : (2 * g + b // 2 + 1) * K]
                        for b in range(4)
                    ]
                )
            )
        )

    loads[7].wait()
    change = []
    for g in range(2):
        rows = slice(g * 128, (g + 1) * 128)
        full = product3(shift_blocks[g], split(inv[rows, :]))
        change.append(jnp.where(ac[rows, :] > 0.5, full, 0.0))
    first = core == 0
    mine_mask = flag(first)
    snd_a[...] = pick(mine_mask, change[1], change[0])
    part[...] = pick(mine_mask, change[0], change[1])

    pl.semaphore_wait(barrier, 4 + (plane - 1) + (planes - 1))

    def remote(src, dst, n, w, o):
        return pltpu.make_async_remote_copy(
            src_ref=src,
            dst_ref=dst,
            send_sem=send_x.at[n],
            recv_sem=recv_x.at[n],
            device_id=at(w, o),
            device_id_type=MESH,
        )

    to_partner = remote(snd_a, rcv_a, 0, me, partner)
    to_partner.start()

    loads[8].wait()
    sla_now = []
    for g in range(2):
        rows = slice(g * 128, (g + 1) * 128)
        high, low = shift_blocks[g]
        taken = oha[rows, :]
        added = product(high, taken, TN) + product(low, taken, TN)
        sla[rows, :] = sla[rows, :] + added

    to_partner.wait_recv()
    part[...] = part[...] + rcv_a[...]
    to_across = remote(part, rcv_b, 1, me, across)
    to_across.start()

    c = [counts[n] for n in range(WD)]
    limit = [c[0]]
    for n in range(1, WD):
        limit.append(limit[-1] + c[n])
    start = [limit[n] - c[n] for n in range(WD)]
    total = limit[-1]

    def copy_masks(j):
        return [flag((start[n] <= j) & (j < limit[n])) for n in range(WD)]

    right_masks = [copy_masks(total - 1), copy_masks(total - 2)]
    left_masks = [copy_masks(jnp.int32(0)), copy_masks(jnp.int32(1))]

    def chosen(masks, parts):
        out = jnp.zeros_like(parts[0])
        for m, x in zip(masks, parts):
            out = pick(m, x, out)
        return out

    sub32 = iota((32, 128), 0)
    lane32 = iota((32, 128), 1)

    @pl.loop(0, WD)
    def _(w):
        ja = jnp.zeros((32, 128), F32)
        sa = jnp.zeros((32, 128), F32)
        for si, sj, weight in ((0, 0, 1.0), (1, 1, 1.0), (0, 1, 2.0)):
            height = jastrow[0 if si == sj else 1]
            falloff = jastrow[2 if si == sj else 3]

            def chunk(n, carry):
                ja, sa = carry
                on = lane32 == sub32 + 32 * n
                old_sq = jnp.zeros((32, 128), F32)
                new_sq = jnp.zeros((32, 128), F32)
                for c in range(3):
                    oi = here[w, 2 * c + si : 2 * c + si + 1, :]
                    oj = here[w, 2 * c + sj : 2 * c + sj + 1, :]
                    ni = misc[w, 2 * c + si : 2 * c + si + 1, :]
                    nj = misc[w, 2 * c + sj : 2 * c + sj + 1, :]
                    oc = jnp.sum(jnp.where(on, oi, 0.0), axis=1, keepdims=True)
                    nc = jnp.sum(jnp.where(on, ni, 0.0), axis=1, keepdims=True)
                    a, e = oc - oj, nc - nj
                    old_sq = old_sq + a * a
                    new_sq = new_sq + e * e
                od, nd = jnp.sqrt(old_sq), jnp.sqrt(new_sq)
                term = nd / (1.0 + falloff * nd) - od / (1.0 + falloff * od)
                soft = 1.0 / jnp.sqrt(new_sq + 1.0)
                return ja + (height * weight) * term, sa + weight * soft

            ja, sa = lax.fori_loop(0, 4, chunk, (ja, sa))
        jt = jnp.sum(jnp.sum(ja, axis=0, keepdims=True), axis=1, keepdims=True)
        st = jnp.sum(jnp.sum(sa, axis=0, keepdims=True), axis=1, keepdims=True)
        energy = (st - 2.0 * NEL) / (2.0 * NEL * (2 * NEL - 1))
        misc[w, 6:7, :] = jnp.broadcast_to(energy, (1, 128))
        misc[w, 7:8, :] = jnp.broadcast_to(jt, (1, 128))

    def pack(dst, masks, parts, n_rows):
        for n in range(2):
            dst[n * n_rows : (n + 1) * n_rows, :] = chosen(masks[n], parts)

    tiles = [misc[n] for n in range(WD)]
    slaters = [sla[n * 64 : (n + 1) * 64, :] for n in range(WD)]
    pack(sla_r, right_masks, slaters, 64)
    pack(sla_l, left_masks, slaters, 64)
    for n in range(2):
        sla_r[128 + 8 * n : 136 + 8 * n, :] = chosen(right_masks[n], tiles)
        sla_l[128 + 8 * n : 136 + 8 * n, :] = chosen(left_masks[n], tiles)
    slater_right = remote(sla_r, rs_l, 3, right, ob)
    slater_left = remote(sla_l, rs_r, 4, left, ob)
    slater_right.start()
    slater_left.start()

    l1 = iota((1, 128), 1)
    weighted = jnp.zeros((1, 128), F32)
    for n in range(WD):
        weighted = weighted + c[n].astype(F32) * tiles[n][6:7, :]
    own = jnp.where(l1 == 0, total.astype(F32), jnp.where(l1 == 1, weighted, 0.0))
    row_a[...] = own

    def in_plane(q):
        return pltpu.make_async_remote_copy(
            src_ref=row_a,
            dst_ref=tab_a.at[r],
            send_sem=send_a.at[q],
            recv_sem=recv_a.at[r],
            device_id=at(z * plane + q, ob),
            device_id_type=MESH,
        )

    def from_plane(q):
        return pltpu.make_async_remote_copy(
            src_ref=row_a,
            dst_ref=tab_a.at[q],
            send_sem=send_a.at[q],
            recv_sem=recv_a.at[q],
            device_id=at(z * plane + q, ob),
            device_id_type=MESH,
        )

    @pl.loop(1, plane)
    def _(t):
        in_plane((r + t) % plane).start()

    column_blocks = []
    block_on = (iota((128, 128), 0) // K) == (iota((128, 128), 1) // K)
    for g in range(2):
        rows = slice(g * 128, (g + 1) * 128)
        high, low = split(inv[rows, :])
        which = oh[rows, :]
        got = product(high, which, NT) + product(low, which, NT)
        column_blocks.append(split(jnp.where(block_on, got, 0.0)))

    to_across.wait_recv()
    summed = part[...] + rcv_b[...]
    high, low = split(summed)
    which = oh[pl.ds(pl.multiple_of(core * 128, 128), 128), :]
    got = product(high, which, NT) + product(low, which, NT)
    lane8 = iota((8, 128), 1)
    sub8 = iota((8, 128), 0)
    seg8 = lane8 // K
    in_seg = lane8 % K
    tile = []
    for t in range(4):
        x = jnp.where(in_seg == sub8 + 8 * t, 1.0, 0.0)
        for b in range(4):
            x = x + jnp.where(seg8 == b, got[b * K + 8 * t : b * K + 8 * t + 8], 0.0)
        tile.append(x)

    def panel(p, carry):
        m, logs = list(carry[:4]), carry[4]
        base = 8 * p
        cols = [
            [jnp.take_along_axis(m[t], seg8 * K + base + n, axis=1) for t in range(4)]
            for n in range(8)
        ]
        pivots = jnp.ones((8, 128), F32)
        for n in range(8):
            bk = cols[n]
            pivot = bk[0][n : n + 1, :]
            inverse_pivot = 1.0 / pivot
            pivots = jnp.where(sub8 == n, pivot, pivots)
            spot = in_seg == base + n
            row = jnp.where(spot, inverse_pivot, m[0][n : n + 1, :] * inverse_pivot)
            for t in range(4):
                fresh = jnp.where(spot, 0.0, m[t]) - bk[t] * row
                m[t] = jnp.where(sub8 == n, row, fresh) if t == 0 else fresh
            for j in range(n + 1, 8):
                scale = cols[j][0][n : n + 1, :] * inverse_pivot
                for t in range(4):
                    fresh = cols[j][t] - bk[t] * scale
                    cols[j][t] = jnp.where(sub8 == n, scale, fresh) if t == 0 else fresh
        logs = logs + jnp.log(jnp.abs(pivots))
        return m[1], m[2], m[3], m[0], logs

    *tile, logs = lax.fori_loop(0, 4, panel, (*tile, jnp.zeros((8, 128), F32)))
    reverse = jnp.concatenate(tile, axis=0)
    solved = product3(split(block_rows([reverse] * 4)), (high, low))
    logdet = jnp.broadcast_to(jnp.sum(logs, axis=0, keepdims=True), (8, 128))
    solv[core, 0:128, :] = solved
    solv[core, 128:136, :] = logdet
    swap = remote(solv.at[core], solv.at[core], 2, me, partner)
    swap.start()

    @pl.loop(1, plane)
    def _(t):
        from_plane((r + t) % plane).wait_recv()

    def table(tab, rows, place, own_row):
        before = jnp.zeros((1, 128), F32)
        every = jnp.zeros((1, 128), F32)
        for n in range(rows):
            x = jnp.where(jnp.full((1, 128), place, jnp.int32) == n, own_row, tab[n])
            before = before + jnp.where(jnp.full((1, 128), place, jnp.int32) > n, x, 0.0)
            every = every + x
        return before, every

    before_a, every_a = table(tab_a, plane, r, own)
    row_b[...] = every_a

    def in_column(q, slot):
        return pltpu.make_async_remote_copy(
            src_ref=row_b,
            dst_ref=tab_b.at[slot],
            send_sem=send_b.at[q],
            recv_sem=recv_b.at[slot],
            device_id=at(q * plane + r, ob),
            device_id_type=MESH,
        )

    @pl.loop(1, planes)
    def _(t):
        in_column((z + t) % planes, z).start()

    swap_in = remote(solv.at[1 - core], solv.at[1 - core], 2, me, partner)
    swap_in.wait_recv()
    for g in range(2):
        rows = slice(g * 128, (g + 1) * 128)
        inv[rows, :] = inv[rows, :] - product3(column_blocks[g], split(solv[g, 0:128, :]))
    for n in range(WD):
        row = solv[n // 2, 128:136, :]
        base = 64 * (n % 2)
        up_down = jnp.where((lane8 == base) | (lane8 == base + K), row, 0.0)
        both = splat(jnp.sum(up_down, axis=1, keepdims=True))
        logt[8 * n : 8 * n + 8, :] = (log_amp[n] + both) + 0.5 * splat(tiles[n][7:8, :])
    inverses = [inv[n * 64 : (n + 1) * 64, :] for n in range(WD)]
    log_tiles = [logt[8 * n : 8 * n + 8, :] for n in range(WD)]
    pack(inv_r, right_masks, inverses, 64)
    pack(inv_l, left_masks, inverses, 64)
    for n in range(2):
        inv_r[128 + 8 * n : 136 + 8 * n, :] = chosen(right_masks[n], log_tiles)
        inv_l[128 + 8 * n : 136 + 8 * n, :] = chosen(left_masks[n], log_tiles)
    inverse_right = remote(inv_r, ri_l, 5, right, ob)
    inverse_left = remote(inv_l, ri_r, 6, left, ob)
    inverse_right.start()
    inverse_left.start()

    @pl.loop(1, planes)
    def _(t):
        q = (z + t) % planes
        in_column(q, q).wait_recv()

    before_b, every_b = table(tab_b, planes, z, every_a)
    out_mean[0] = jnp.sum(jnp.where(l1 == 1, every_b, 0.0)) / (WD * walkers)
    ahead = jnp.where(l1 == 0, before_a + before_b, 0.0)
    over = splat(jnp.sum(ahead, axis=1, keepdims=True)) - (WD * me).astype(F32)

    slater_right.wait_recv()
    slater_left.wait_recv()
    inverse_right.wait_recv()
    inverse_left.wait_recv()

    totalf = total.astype(F32)
    for i in range(WD):
        j = i - over
        masks = [j == -1.0, j == -2.0]
        masks += [
            (j >= start[n].astype(F32)) & (j < limit[n].astype(F32)) for n in range(WD)
        ]
        masks += [j == totalf, j == totalf + 1.0]

        def halo(ref_l, ref_r, n_rows, base):
            return [ref_l[base + n * n_rows : base + (n + 1) * n_rows, :] for n in range(2)], [
                ref_r[base + n * n_rows : base + (n + 1) * n_rows, :] for n in range(2)
            ]

        def select(own_parts, ref_l, ref_r, n_rows, base):
            a, e = halo(ref_l, ref_r, n_rows, base)
            return chosen(masks, a + own_parts + e)

        out_inv[i * 64 : (i + 1) * 64, :] = select(
            [inv[n * 64 : (n + 1) * 64, :] for n in range(WD)], ri_l, ri_r, 64, 0
        )
        out_sla[i * 64 : (i + 1) * 64, :] = select(
            [sla[n * 64 : (n + 1) * 64, :] for n in range(WD)], rs_l, rs_r, 64, 0
        )
        small = select([misc[n] for n in range(WD)], rs_l, rs_r, 8, 128)
        logs_here = select(
            [logt[8 * n : 8 * n + 8, :] for n in range(WD)], ri_l, ri_r, 8, 128
        )
        for c3 in range(3):
            for s in range(2):
                out_pos[c3, i : i + 1, s * NEL : (s + 1) * NEL] = small[2 * c3 + s : 2 * c3 + s + 1]
        out_en[i] = small[6, 0]
        out_log[i] = logs_here[0, 0]

    for copy in (
        to_partner,
        to_across,
        swap,
        slater_right,
        slater_left,
        inverse_right,
        inverse_left,
    ):
        copy.wait_send()

    @pl.loop(1, plane)
    def _(t):
        in_plane((r + t) % plane).wait_send()

    @pl.loop(1, planes)
    def _(t):
        in_column((z + t) % planes, z).wait_send()


def solution(mesh):
    walkers = mesh.shape["walkers"]
    plane = 16 if walkers == 128 else walkers // 2
    planes = walkers // plane

    def body(
        inverse,
        slater,
        positions,
        displacements,
        move_order,
        accepted,
        counts,
        log_amp,
        centers,
        exponents,
        orbitals,
        jastrow,
    ):
        smem = pl.BlockSpec(memory_space=pltpu.SMEM)
        vmem = pl.BlockSpec(memory_space=pltpu.VMEM)
        hbm = pl.BlockSpec(memory_space=pl.ANY)

        def shape(*dims):
            return jax.ShapeDtypeStruct(dims, F32)

        def buf(*dims, kind=F32):
            return pltpu.VMEM(dims, kind)

        dma = pltpu.SemaphoreType.DMA
        outs = pl.pallas_call(
            lambda *refs: kernel(planes, plane, *refs),
            out_shape=(
                shape(256, 128),
                shape(256, 128),
                shape(3, 4, 256),
                shape(4),
                shape(4),
                shape(1),
            ),
            in_specs=[smem] * 3 + [hbm] * 9,
            out_specs=(vmem, vmem, vmem, smem, smem, smem),
            scratch_shapes=[
                buf(256, 128),
                buf(256, 128),
                buf(3, 4, 256),
                buf(3, 4, 256),
                buf(8, 128, kind=jnp.int32),
                buf(8, 32, kind=jnp.int32),
                buf(3, 1024),
                buf(8, 128),
                buf(2, 32, 1024),
                buf(2, 128, 1024, kind=BF16),
                buf(2, 128, 1024, kind=BF16),
                buf(256, 128, kind=BF16),
                buf(256, 128, kind=BF16),
                buf(256, 128),
                buf(4, 8, 128),
                buf(4, 16, 128),
                buf(32, 128),
                buf(128, 128),
                buf(128, 128),
                buf(128, 128),
                buf(128, 128),
                buf(2, 136, 128),
                *[buf(144, 128) for _ in range(8)],
                buf(1, 128),
                buf(1, 128),
                buf(plane, 1, 128),
                buf(planes, 1, 128),
                dma((9,)),
                dma((7,)),
                dma((7,)),
                dma((plane,)),
                dma((plane,)),
                dma((planes,)),
                dma((planes,)),
            ],
            compiler_params=pltpu.CompilerParams(collective_id=0, has_side_effects=True),
            name="generation",
        )(
            counts,
            jastrow,
            log_amp,
            inverse.reshape(256, 128),
            slater.reshape(256, 128),
            positions.transpose(1, 0, 2),
            displacements.transpose(1, 0, 2),
            move_order.reshape(8, 128),
            accepted.reshape(8, 32),
            centers,
            exponents.reshape(8, 128),
            orbitals,
        )
        return (
            outs[0].reshape(4, 2, 32, 128),
            outs[1].reshape(4, 2, 32, 128),
            outs[2].transpose(1, 0, 2),
            outs[3],
            outs[4],
            outs[5].reshape(()),
        )

    placed = (
        P("walkers", None, "orb", None),
        P("walkers", None, "orb", None),
        P("walkers", None, None),
        P("walkers", None, None),
        P("walkers", None, None),
        P("walkers", None, None),
        P("walkers"),
        P("walkers"),
        P(),
        P(),
        P(None, "orb", None),
        P(),
    )
    return jax.shard_map(
        body,
        mesh=mesh,
        in_specs=placed,
        out_specs=(
            P("walkers", None, "orb", None),
            P("walkers", None, "orb", None),
            P("walkers", None, None),
            P("walkers"),
            P("walkers"),
            P(),
        ),
        check_vma=False,
    )
```

time: 238 us -> 46.1 us (0.19)
  the two profiles are of different devices: /device:TPU:11 before, /device:TPU:1 now
where the time goes in v1:
time: 46.1 us; the launch traced here: 45.8 us
  Pallas kernels  39.4 us (85%)
  local copies, waits for them, and re-layouts  4.07 us (9%)
  between operations  2.41 us (5%)
    pallas_call x1, Pallas kernels, body(): pl.pallas_call(lambda *refs: kernel(planes, plane, *refs), out_shape=(sha...  39.4 us
    unnamed x13, local copies, waits for them, and re-layouts  4.07 us

profile of v1, /device:TPU:1, one launch (start us, length us, event | category | flops | bytes accessed | tf_op | source)
XLA Modules:
  0.0 45.8 jit_solution(7642172439786980424)
XLA Ops:
  0.6 39.4 %generation.1 = (f32[256,128]{1,0:T(8,128)}, f32[256,128]{1,0:T(8,128)}, f32[3,4,256]{2,1,0:T(4,128)}, f32[4]{0:T(128)}, f32[4]{0:T(128)}, /*index=5*/f32[1]{0:T(128)}) custom-call(s32[4]{0:T(128)} %refs_0_.1, f32[4]{0:T(128)} %refs_1_.1, f32[4]{0:T(128)} %refs_2_.1, f32[256,128]{1,0:T(8,128)} %bitcast.13, f32[256,128]{1,0:T(8,128)} %bitcast.14, ...), custom_call_target="tpu_custom_call" | custom-call | tf_op jit(solution)/shard_map/generation/pallas_call | solution.py:609
  40.0 0.0 copy-start
  40.0 1.6 %copy.24 = f32[4,2,32,128]{3,2,1,0:T(8,128)} copy(f32[4,2,32,128]{3,2,1,0:T(8,128)} %bitcast.12) | data formatting | bytes 262144
  41.6 0.0 copy-done
  41.6 0.0 copy-start.1
  41.6 0.7 %copy.25 = f32[4,2,32,128]{3,2,1,0:T(8,128)} copy(f32[4,2,32,128]{3,2,1,0:T(8,128)S(1)} %bitcast.11) | data formatting | bytes 262144
  42.3 0.0 copy-done.1
  42.3 0.0 copy-start.3
  42.3 0.6 %copy.26 = f32[4,3,256]{2,0,1:T(4,128)} copy(f32[4,3,256]{2,0,1:T(4,128)S(1)} %bitcast.15) | data formatting | bytes 24576
  42.9 0.0 copy-done.3
  42.9 0.0 copy-start.2
  42.9 0.5 %copy.27 = f32[4]{0:T(128)} copy(f32[4]{0:T(128)S(1)} %copy-done.3) | data formatting | bytes 32
  43.5 0.1 copy-done.2
  43.6 0.5 %copy.28 = f32[4]{0:T(128)} copy(f32[4]{0:T(128)S(1)} %copy-done.2) | data formatting | bytes 32
Async XLA Ops:
  40.0 1.6 %copy-start = (f32[256,128]{1,0:T(8,128)S(1)}, f32[256,128]{1,0:T(8,128)}, u32[]{:S(2)}) copy-start(f32[256,128]{1,0:T(8,128)} %get-tuple-element.13) | copy-start | bytes 393220
  41.6 0.7 %copy-start.1 = (f32[3,4,256]{2,1,0:T(4,128)S(1)}, f32[3,4,256]{2,1,0:T(4,128)}, u32[]{:S(2)}) copy-start(f32[3,4,256]{2,1,0:T(4,128)} %get-tuple-element.14) | copy-start | bytes 36868
  42.3 0.6 %copy-start.3 = (f32[4]{0:T(128)S(1)}, f32[4]{0:T(128)}, u32[]{:S(2)}) copy-start(f32[4]{0:T(128)} %get-tuple-element.27) | copy-start | bytes 52
  42.9 0.6 %copy-start.2 = (f32[4]{0:T(128)S(1)}, f32[4]{0:T(128)}, u32[]{:S(2)}) copy-start(f32[4]{0:T(128)} %get-tuple-element.28) | copy-start | bytes 52

commit v2 on v1

--- a/solution.py
+++ b/solution.py
@@ -57,9 +57,9 @@
 def kernel(
     planes,
     plane,
-    counts,
-    jastrow,
-    log_amp,
+    cnt_hbm,
+    jas_hbm,
+    amp_hbm,
     inv_hbm,
     sla_hbm,
     pos_hbm,
@@ -69,12 +69,10 @@
     cen_hbm,
     ex_hbm,
     orb_hbm,
-    out_inv,
-    out_sla,
-    out_pos,
-    out_log,
-    out_en,
-    out_mean,
+    out,
+    counts,
+    jastrow,
+    log_amp,
     inv,
     sla,
     pos,
@@ -91,6 +89,7 @@
     ac,
     misc,
     here,
+    pts,
     logt,
     snd_a,
     part,
@@ -123,30 +122,10 @@
     core = ob % 2
     partner = (ob // 2) * 2 + (1 - core)
     across = (1 - ob // 2) * 2 + core
-    right = (me + 1) % walkers
-    left = (me + walkers - 1) % walkers
     z, r = me // plane, me % plane
 
     def at(w, o):
         return {"walkers": w, "orb": o}
-
-    barrier = pltpu.get_barrier_semaphore()
-
-    def greet(w, o):
-        pl.semaphore_signal(barrier, inc=1, device_id=at(w, o), device_id_type=MESH)
-
-    greet(me, partner)
-    greet(me, across)
-    greet(right, ob)
-    greet(left, ob)
-
-    @pl.loop(1, plane)
-    def _(t):
-        greet(z * plane + (r + t) % plane, ob)
-
-    @pl.loop(1, planes)
-    def _(t):
-        greet(((z + t) % planes) * plane + r, ob)
 
     loads = [
         pltpu.make_async_copy(src, dst, in_sem.at[n])
@@ -161,11 +140,49 @@
                 (orb_hbm, orb),
                 (inv_hbm, inv),
                 (sla_hbm, sla),
+                (cnt_hbm, counts),
+                (jas_hbm, jastrow),
+                (amp_hbm, log_amp),
             )
         )
     ]
     for load in loads:
         load.start()
+    barrier = pltpu.get_barrier_semaphore()
+
+    def greet(w, o):
+        pl.semaphore_signal(barrier, inc=1, device_id=at(w, o), device_id_type=MESH)
+
+    greet(me, partner)
+    greet(me, across)
+    has_right, has_left = me < walkers - 1, me > 0
+
+    @pl.when(has_right)
+    def _():
+        greet(me + 1, ob)
+
+    @pl.when(has_left)
+    def _():
+        greet(me - 1, ob)
+
+    @pl.when(me == 0)
+    def _():
+        rs_l[...] = jnp.zeros_like(rs_l)
+        ri_l[...] = jnp.zeros_like(ri_l)
+
+    @pl.when(me == walkers - 1)
+    def _():
+        rs_r[...] = jnp.zeros_like(rs_r)
+        ri_r[...] = jnp.zeros_like(ri_r)
+
+    @pl.loop(1, plane)
+    def _(t):
+        greet(z * plane + (r + t) % plane, ob)
+
+    @pl.loop(1, planes)
+    def _(t):
+        greet(((z + t) % planes) * plane + r, ob)
+
     for load in loads[:6]:
         load.wait()
 
@@ -203,8 +220,70 @@
             old.append(jnp.sum(one * p, axis=1, keepdims=True))
             new.append(jnp.sum(one * (p + d), axis=1, keepdims=True))
             misc[w, pl.ds(2 * c + s, 1), :] = p + d * applied
-        old = [jnp.broadcast_to(v, (K, 128)) for v in old]
-        new = [jnp.broadcast_to(v, (K, 128)) for v in new]
+        for c in range(3):
+            pts[c, rows, :] = jnp.broadcast_to(old[c], (K, 128))
+            pts[c + 3, rows, :] = jnp.broadcast_to(new[c], (K, 128))
+
+    for load in loads[9:]:
+        load.wait()
+    sub32 = iota((32, 128), 0)
+
+    @pl.loop(0, WD)
+    def _(w):
+        zero = jnp.zeros((32, 128), F32)
+        js, jd, es, ed = zero, zero, zero, zero
+
+        def pair_block(oc, nc, sj, falloff, ja, ea):
+            old_sq, new_sq = zero, zero
+            for c in range(3):
+                a = oc[c] - here[w, 2 * c + sj : 2 * c + sj + 1, :]
+                e = nc[c] - misc[w, 2 * c + sj : 2 * c + sj + 1, :]
+                old_sq = old_sq + a * a
+                new_sq = new_sq + e * e
+            od, nd = jnp.sqrt(old_sq), jnp.sqrt(new_sq)
+            term = (nd - od) / ((1.0 + falloff * nd) * (1.0 + falloff * od))
+            return ja + term, ea + lax.rsqrt(new_sq + 1.0)
+
+        for si in range(2):
+            for n in range(4):
+                on = lane == sub32 + 32 * n
+                oc, nc = [], []
+                for c in range(3):
+                    oi = here[w, 2 * c + si : 2 * c + si + 1, :]
+                    ni = misc[w, 2 * c + si : 2 * c + si + 1, :]
+                    oc.append(jnp.sum(jnp.where(on, oi, 0.0), axis=1, keepdims=True))
+                    nc.append(jnp.sum(jnp.where(on, ni, 0.0), axis=1, keepdims=True))
+                js, es = pair_block(oc, nc, si, jastrow[2], js, es)
+                if si == 0:
+                    jd, ed = pair_block(oc, nc, 1, jastrow[3], jd, ed)
+        ja = jastrow[0] * js + (2.0 * jastrow[1]) * jd
+        ea = es + 2.0 * ed
+        jt = jnp.sum(jnp.sum(ja, axis=0, keepdims=True), axis=1, keepdims=True)
+        st = jnp.sum(jnp.sum(ea, axis=0, keepdims=True), axis=1, keepdims=True)
+        energy = (st - 2.0 * NEL) / (2.0 * NEL * (2 * NEL - 1))
+        misc[w, 6:7, :] = jnp.broadcast_to(energy, (1, 128))
+        misc[w, 7:8, :] = jnp.broadcast_to(jt, (1, 128))
+
+    l1 = iota((1, 128), 1)
+    c = [counts[n] for n in range(WD)]
+    limit = [c[0]]
+    for n in range(1, WD):
+        limit.append(limit[-1] + c[n])
+    start = [limit[n] - c[n] for n in range(WD)]
+    total = limit[-1]
+    tiles = [misc[n] for n in range(WD)]
+    weighted = jnp.zeros((1, 128), F32)
+    for n in range(WD):
+        weighted = weighted + c[n].astype(F32) * tiles[n][6:7, :]
+    own = jnp.where(l1 == 0, total.astype(F32), jnp.where(l1 == 1, weighted, 0.0))
+    row_a[...] = own
+
+    @pl.loop(0, 2 * WD)
+    def _(b):
+        w, s = b // 2, b % 2
+        rows = pl.ds(pl.multiple_of(b * K, K), K)
+        old = [pts[c, rows, :] for c in range(3)]
+        new = [pts[c + 3, rows, :] for c in range(3)]
         to = pl.ds(pl.multiple_of(w * K, K), K)
         for n in range(8):
             span = slice(n * 128, (n + 1) * 128)
@@ -261,7 +340,8 @@
     snd_a[...] = pick(mine_mask, change[1], change[0])
     part[...] = pick(mine_mask, change[0], change[1])
 
-    pl.semaphore_wait(barrier, 4 + (plane - 1) + (planes - 1))
+    neighbours = jnp.where(has_right, 1, 0) + jnp.where(has_left, 1, 0)
+    pl.semaphore_wait(barrier, 2 + (plane - 1) + (planes - 1) + neighbours)
 
     def remote(src, dst, n, w, o):
         return pltpu.make_async_remote_copy(
@@ -276,6 +356,31 @@
     to_partner = remote(snd_a, rcv_a, 0, me, partner)
     to_partner.start()
 
+    def in_plane(q):
+        return pltpu.make_async_remote_copy(
+            src_ref=row_a,
+            dst_ref=tab_a.at[r],
+            send_sem=send_a.at[q],
+            recv_sem=recv_a.at[r],
+            device_id=at(z * plane + q, ob),
+            device_id_type=MESH,
+        )
+
+    def from_plane(q):
+        return pltpu.make_async_remote_copy(
+            src_ref=row_a,
+            dst_ref=tab_a.at[q],
+            send_sem=send_a.at[q],
+            recv_sem=recv_a.at[q],
+            device_id=at(z * plane + q, ob),
+            device_id_type=MESH,
+        )
+
+    @pl.loop(1, plane)
+    def _(t):
+        in_plane((r + t) % plane).start()
+
+
     loads[8].wait()
     sla_now = []
     for g in range(2):
@@ -290,13 +395,6 @@
     to_across = remote(part, rcv_b, 1, me, across)
     to_across.start()
 
-    c = [counts[n] for n in range(WD)]
-    limit = [c[0]]
-    for n in range(1, WD):
-        limit.append(limit[-1] + c[n])
-    start = [limit[n] - c[n] for n in range(WD)]
-    total = limit[-1]
-
     def copy_masks(j):
         return [flag((start[n] <= j) & (j < limit[n])) for n in range(WD)]
 
@@ -309,90 +407,16 @@
             out = pick(m, x, out)
         return out
 
-    sub32 = iota((32, 128), 0)
-    lane32 = iota((32, 128), 1)
-
-    @pl.loop(0, WD)
-    def _(w):
-        ja = jnp.zeros((32, 128), F32)
-        sa = jnp.zeros((32, 128), F32)
-        for si, sj, weight in ((0, 0, 1.0), (1, 1, 1.0), (0, 1, 2.0)):
-            height = jastrow[0 if si == sj else 1]
-            falloff = jastrow[2 if si == sj else 3]
-
-            def chunk(n, carry):
-                ja, sa = carry
-                on = lane32 == sub32 + 32 * n
-                old_sq = jnp.zeros((32, 128), F32)
-                new_sq = jnp.zeros((32, 128), F32)
-                for c in range(3):
-                    oi = here[w, 2 * c + si : 2 * c + si + 1, :]
-                    oj = here[w, 2 * c + sj : 2 * c + sj + 1, :]
-                    ni = misc[w, 2 * c + si : 2 * c + si + 1, :]
-                    nj = misc[w, 2 * c + sj : 2 * c + sj + 1, :]
-                    oc = jnp.sum(jnp.where(on, oi, 0.0), axis=1, keepdims=True)
-                    nc = jnp.sum(jnp.where(on, ni, 0.0), axis=1, keepdims=True)
-                    a, e = oc - oj, nc - nj
-                    old_sq = old_sq + a * a
-                    new_sq = new_sq + e * e
-                od, nd = jnp.sqrt(old_sq), jnp.sqrt(new_sq)
-                term = nd / (1.0 + falloff * nd) - od / (1.0 + falloff * od)
-                soft = 1.0 / jnp.sqrt(new_sq + 1.0)
-                return ja + (height * weight) * term, sa + weight * soft
-
-            ja, sa = lax.fori_loop(0, 4, chunk, (ja, sa))
-        jt = jnp.sum(jnp.sum(ja, axis=0, keepdims=True), axis=1, keepdims=True)
-        st = jnp.sum(jnp.sum(sa, axis=0, keepdims=True), axis=1, keepdims=True)
-        energy = (st - 2.0 * NEL) / (2.0 * NEL * (2 * NEL - 1))
-        misc[w, 6:7, :] = jnp.broadcast_to(energy, (1, 128))
-        misc[w, 7:8, :] = jnp.broadcast_to(jt, (1, 128))
-
     def pack(dst, masks, parts, n_rows):
         for n in range(2):
             dst[n * n_rows : (n + 1) * n_rows, :] = chosen(masks[n], parts)
 
-    tiles = [misc[n] for n in range(WD)]
     slaters = [sla[n * 64 : (n + 1) * 64, :] for n in range(WD)]
     pack(sla_r, right_masks, slaters, 64)
     pack(sla_l, left_masks, slaters, 64)
     for n in range(2):
         sla_r[128 + 8 * n : 136 + 8 * n, :] = chosen(right_masks[n], tiles)
         sla_l[128 + 8 * n : 136 + 8 * n, :] = chosen(left_masks[n], tiles)
-    slater_right = remote(sla_r, rs_l, 3, right, ob)
-    slater_left = remote(sla_l, rs_r, 4, left, ob)
-    slater_right.start()
-    slater_left.start()
-
-    l1 = iota((1, 128), 1)
-    weighted = jnp.zeros((1, 128), F32)
-    for n in range(WD):
-        weighted = weighted + c[n].astype(F32) * tiles[n][6:7, :]
-    own = jnp.where(l1 == 0, total.astype(F32), jnp.where(l1 == 1, weighted, 0.0))
-    row_a[...] = own
-
-    def in_plane(q):
-        return pltpu.make_async_remote_copy(
-            src_ref=row_a,
-            dst_ref=tab_a.at[r],
-            send_sem=send_a.at[q],
-            recv_sem=recv_a.at[r],
-            device_id=at(z * plane + q, ob),
-            device_id_type=MESH,
-        )
-
-    def from_plane(q):
-        return pltpu.make_async_remote_copy(
-            src_ref=row_a,
-            dst_ref=tab_a.at[q],
-            send_sem=send_a.at[q],
-            recv_sem=recv_a.at[q],
-            device_id=at(z * plane + q, ob),
-            device_id_type=MESH,
-        )
-
-    @pl.loop(1, plane)
-    def _(t):
-        in_plane((r + t) % plane).start()
 
     column_blocks = []
     block_on = (iota((128, 128), 0) // K) == (iota((128, 128), 1) // K)
@@ -403,7 +427,20 @@
         got = product(high, which, NT) + product(low, which, NT)
         column_blocks.append(split(jnp.where(block_on, got, 0.0)))
 
+    slater_right = remote(sla_r, rs_l, 3, me + 1, ob)
+    slater_left = remote(sla_l, rs_r, 4, me - 1, ob)
+
+    def start_both(to_right, to_left):
+        @pl.when(has_right)
+        def _():
+            to_right.start()
+
+        @pl.when(has_left)
+        def _():
+            to_left.start()
+
     to_across.wait_recv()
+    start_both(slater_right, slater_left)
     summed = part[...] + rcv_b[...]
     high, low = split(summed)
     which = oh[pl.ds(pl.multiple_of(core * 128, 128), 128), :]
@@ -454,36 +491,6 @@
     swap = remote(solv.at[core], solv.at[core], 2, me, partner)
     swap.start()
 
-    @pl.loop(1, plane)
-    def _(t):
-        from_plane((r + t) % plane).wait_recv()
-
-    def table(tab, rows, place, own_row):
-        before = jnp.zeros((1, 128), F32)
-        every = jnp.zeros((1, 128), F32)
-        for n in range(rows):
-            x = jnp.where(jnp.full((1, 128), place, jnp.int32) == n, own_row, tab[n])
-            before = before + jnp.where(jnp.full((1, 128), place, jnp.int32) > n, x, 0.0)
-            every = every + x
-        return before, every
-
-    before_a, every_a = table(tab_a, plane, r, own)
-    row_b[...] = every_a
-
-    def in_column(q, slot):
-        return pltpu.make_async_remote_copy(
-            src_ref=row_b,
-            dst_ref=tab_b.at[slot],
-            send_sem=send_b.at[q],
-            recv_sem=recv_b.at[slot],
-            device_id=at(q * plane + r, ob),
-            device_id_type=MESH,
-        )
-
-    @pl.loop(1, planes)
-    def _(t):
-        in_column((z + t) % planes, z).start()
-
     swap_in = remote(solv.at[1 - core], solv.at[1 - core], 2, me, partner)
     swap_in.wait_recv()
     for g in range(2):
@@ -502,10 +509,39 @@
     for n in range(2):
         inv_r[128 + 8 * n : 136 + 8 * n, :] = chosen(right_masks[n], log_tiles)
         inv_l[128 + 8 * n : 136 + 8 * n, :] = chosen(left_masks[n], log_tiles)
-    inverse_right = remote(inv_r, ri_l, 5, right, ob)
-    inverse_left = remote(inv_l, ri_r, 6, left, ob)
-    inverse_right.start()
-    inverse_left.start()
+    inverse_right = remote(inv_r, ri_l, 5, me + 1, ob)
+    inverse_left = remote(inv_l, ri_r, 6, me - 1, ob)
+    start_both(inverse_right, inverse_left)
+
+    @pl.loop(1, plane)
+    def _(t):
+        from_plane((r + t) % plane).wait_recv()
+
+    def table(tab, rows, place, own_row):
+        before = jnp.zeros((1, 128), F32)
+        every = jnp.zeros((1, 128), F32)
+        for n in range(rows):
+            x = jnp.where(jnp.full((1, 128), place, jnp.int32) == n, own_row, tab[n])
+            before = before + jnp.where(jnp.full((1, 128), place, jnp.int32) > n, x, 0.0)
+            every = every + x
+        return before, every
+
+    before_a, every_a = table(tab_a, plane, r, own)
+    row_b[...] = every_a
+
+    def in_column(q, slot):
+        return pltpu.make_async_remote_copy(
+            src_ref=row_b,
+            dst_ref=tab_b.at[slot],
+            send_sem=send_b.at[q],
+            recv_sem=recv_b.at[slot],
+            device_id=at(q * plane + r, ob),
+            device_id_type=MESH,
+        )
+
+    @pl.loop(1, planes)
+    def _(t):
+        in_column((z + t) % planes, z).start()
 
     @pl.loop(1, planes)
     def _(t):
@@ -513,14 +549,20 @@
         in_column(q, q).wait_recv()
 
     before_b, every_b = table(tab_b, planes, z, every_a)
-    out_mean[0] = jnp.sum(jnp.where(l1 == 1, every_b, 0.0)) / (WD * walkers)
+    mean = jnp.sum(jnp.where(l1 == 1, every_b, 0.0), axis=1, keepdims=True)
+    out[552:560, :] = splat(mean) / (WD * walkers)
     ahead = jnp.where(l1 == 0, before_a + before_b, 0.0)
     over = splat(jnp.sum(ahead, axis=1, keepdims=True)) - (WD * me).astype(F32)
 
-    slater_right.wait_recv()
-    slater_left.wait_recv()
-    inverse_right.wait_recv()
-    inverse_left.wait_recv()
+    @pl.when(has_left)
+    def _():
+        slater_right.wait_recv()
+        inverse_right.wait_recv()
+
+    @pl.when(has_right)
+    def _():
+        slater_left.wait_recv()
+        inverse_left.wait_recv()
 
     totalf = total.astype(F32)
     for i in range(WD):
@@ -540,32 +582,38 @@
             a, e = halo(ref_l, ref_r, n_rows, base)
             return chosen(masks, a + own_parts + e)
 
-        out_inv[i * 64 : (i + 1) * 64, :] = select(
+        out[i * 64 : (i + 1) * 64, :] = select(
             [inv[n * 64 : (n + 1) * 64, :] for n in range(WD)], ri_l, ri_r, 64, 0
         )
-        out_sla[i * 64 : (i + 1) * 64, :] = select(
+        out[256 + i * 64 : 256 + (i + 1) * 64, :] = select(
             [sla[n * 64 : (n + 1) * 64, :] for n in range(WD)], rs_l, rs_r, 64, 0
         )
         small = select([misc[n] for n in range(WD)], rs_l, rs_r, 8, 128)
         logs_here = select(
             [logt[8 * n : 8 * n + 8, :] for n in range(WD)], ri_l, ri_r, 8, 128
         )
-        for c3 in range(3):
-            for s in range(2):
-                out_pos[c3, i : i + 1, s * NEL : (s + 1) * NEL] = small[2 * c3 + s : 2 * c3 + s + 1]
-        out_en[i] = small[6, 0]
-        out_log[i] = logs_here[0, 0]
+        for n in range(6):
+            row = 512 + 4 * n + i
+            out[row : row + 1, :] = small[n : n + 1, :]
+        out[536 + i : 537 + i, :] = logs_here[0:1, :]
+        out[544 + i : 545 + i, :] = small[6:7, :]
 
     for copy in (
         to_partner,
         to_across,
         swap,
-        slater_right,
-        slater_left,
-        inverse_right,
-        inverse_left,
     ):
         copy.wait_send()
+
+    @pl.when(has_right)
+    def _():
+        slater_right.wait_send()
+        inverse_right.wait_send()
+
+    @pl.when(has_left)
+    def _():
+        slater_left.wait_send()
+        inverse_left.wait_send()
 
     @pl.loop(1, plane)
     def _(t):
@@ -574,6 +622,20 @@
     @pl.loop(1, planes)
     def _(t):
         in_column((z + t) % planes, z).wait_send()
+
+
+def finish(packed, out_inv, out_sla, out_pos, out_log, out_en, out_mean):
+    out_inv[...] = packed[0:256, :]
+    out_sla[...] = packed[256:512, :]
+    for c in range(3):
+        for s in range(2):
+            row = 512 + 8 * c + 4 * s
+            out_pos[c, :, s * NEL : (s + 1) * NEL] = packed[row : row + 4, :]
+    logs, energies = packed[536:544, :], packed[544:552, :]
+    for i in range(WD):
+        out_log[i] = logs[i, 0]
+        out_en[i] = energies[i, 0]
+    out_mean[0] = packed[552:560, :][0, 0]
 
 
 def solution(mesh):
@@ -597,7 +659,7 @@
     ):
         smem = pl.BlockSpec(memory_space=pltpu.SMEM)
         vmem = pl.BlockSpec(memory_space=pltpu.VMEM)
-        hbm = pl.BlockSpec(memory_space=pl.ANY)
+        hbm = pl.BlockSpec(memory_space=pltpu.HBM)
 
         def shape(*dims):
             return jax.ShapeDtypeStruct(dims, F32)
@@ -606,19 +668,15 @@
             return pltpu.VMEM(dims, kind)
 
         dma = pltpu.SemaphoreType.DMA
-        outs = pl.pallas_call(
+        packed = pl.pallas_call(
             lambda *refs: kernel(planes, plane, *refs),
-            out_shape=(
-                shape(256, 128),
-                shape(256, 128),
-                shape(3, 4, 256),
-                shape(4),
-                shape(4),
-                shape(1),
-            ),
-            in_specs=[smem] * 3 + [hbm] * 9,
-            out_specs=(vmem, vmem, vmem, smem, smem, smem),
+            out_shape=shape(560, 128),
+            in_specs=[hbm] * 12,
+            out_specs=vmem,
             scratch_shapes=[
+                pltpu.SMEM((4,), jnp.int32),
+                pltpu.SMEM((4,), F32),
+                pltpu.SMEM((4,), F32),
                 buf(256, 128),
                 buf(256, 128),
                 buf(3, 4, 256),
@@ -635,6 +693,7 @@
                 buf(256, 128),
                 buf(4, 8, 128),
                 buf(4, 16, 128),
+                buf(6, 256, 128),
                 buf(32, 128),
                 buf(128, 128),
                 buf(128, 128),
@@ -646,7 +705,7 @@
                 buf(1, 128),
                 buf(plane, 1, 128),
                 buf(planes, 1, 128),
-                dma((9,)),
+                dma((12,)),
                 dma((7,)),
                 dma((7,)),
                 dma((plane,)),
@@ -654,9 +713,11 @@
                 dma((planes,)),
                 dma((planes,)),
             ],
-            compiler_params=pltpu.CompilerParams(collective_id=0, has_side_effects=True),
+            compiler_params=pltpu.CompilerParams(
+                collective_id=0, has_side_effects=True, vmem_limit_bytes=16 << 20
+            ),
             name="generation",
-        )(
+        )(*[pltpu.with_memory_space_constraint(x, pltpu.HBM) for x in (
             counts,
             jastrow,
             log_amp,
@@ -669,7 +730,22 @@
             centers,
             exponents.reshape(8, 128),
             orbitals,
-        )
+        )])
+        outs = pl.pallas_call(
+            finish,
+            out_shape=(
+                shape(256, 128),
+                shape(256, 128),
+                shape(3, 4, 256),
+                shape(4),
+                shape(4),
+                shape(1),
+            ),
+            in_specs=[vmem],
+            out_specs=(vmem, vmem, vmem, smem, smem, smem),
+            compiler_params=pltpu.CompilerParams(vmem_limit_bytes=4 << 20),
+            name="finish",
+        )(packed)
         return (
             outs[0].reshape(4, 2, 32, 128),
             outs[1].reshape(4, 2, 32, 128),

time: 46.1 us -> 28.9 us (0.63)
  Pallas kernels: 39.4 us -> 28.1 us
  local copies, waits for them, and re-layouts: 4.07 us -> 0 us
  between operations: 2.41 us -> 0.65 us
    pallas_call x1 -> x2, Pallas kernels: 39.4 us -> 28.1 us  [the longest x1 27.4 us: body(): pl.pallas_call(lambda *refs: kernel(planes, plane, *refs), out_shape=shap...]
    unnamed x13 -> x0, local copies, waits for them, and re-layouts: 4.07 us -> none
where the time goes in v2:
time: 28.9 us; the launch traced here: 28.8 us
  Pallas kernels  28.1 us (97%)
  between operations  0.65 us (2%)
    pallas_call x1, Pallas kernels, body(): pl.pallas_call(lambda *refs: kernel(planes, plane, *refs), out_shape=shap...  27.4 us
    pallas_call x1, Pallas kernels, body(): pl.pallas_call(finish, out_shape=(shape(256, 128), shape(256, 128), shape...  0.73 us

profile of v2, /device:TPU:1, one launch (start us, length us, event | category | flops | bytes accessed | tf_op | source)
XLA Modules:
  0.0 28.8 jit_solution(4354289014438097951)
XLA Ops:
  0.6 27.4 %generation.1.packed = f32[560,128]{1,0:T(8,128)S(1)} custom-call(s32[4]{0:T(128)} %refs_0_.1, f32[4]{0:T(128)} %refs_1_.1, f32[4]{0:T(128)} %refs_2_.1, f32[256,128]{1,0:T(8,128)} %bitcast.11, f32[256,128]{1,0:T(8,128)} %bitcast.12, f32[3,4,256]{2,1,0:T(4,128)} %bitcast.13, f32[3,4,256]{2,1,0:T(4,128)} %bitcast.14, s32[8,128]{1,0:T(8,128)} %bitcast.15, ...), custom_call_target="tpu_custom_call" | custom-call | tf_op jit(solution)/shard_map/generation/pallas_call | solution.py:671
  28.0 0.7 %finish.1 = (f32[256,128]{1,0:T(8,128)}, f32[256,128]{1,0:T(8,128)}, f32[3,4,256]{2,1,0:T(4,128)}, f32[4]{0:T(128)}, f32[4]{0:T(128)}, /*index=5*/f32[1]{0:T(128)}) custom-call(f32[560,128]{1,0:T(8,128)S(1)} %generation.1.packed), custom_call_target="tpu_custom_call" | custom-call | tf_op jit(solution)/shard_map/finish/pallas_call | solution.py:734

commit v3 on v2

--- a/solution.py
+++ b/solution.py
@@ -106,6 +106,7 @@
     ri_l,
     row_a,
     row_b,
+    pre,
     tab_a,
     tab_b,
     in_sem,
@@ -115,6 +116,7 @@
     recv_a,
     send_b,
     recv_b,
+    up_sem,
 ):
     me = lax.axis_index("walkers")
     ob = lax.axis_index("orb")
@@ -126,6 +128,31 @@
 
     def at(w, o):
         return {"walkers": w, "orb": o}
+
+    barrier = pltpu.get_barrier_semaphore()
+
+    def greet(w, o):
+        pl.semaphore_signal(barrier, inc=1, device_id=at(w, o), device_id_type=MESH)
+
+    greet(me, partner)
+    greet(me, across)
+    has_right, has_left = me < walkers - 1, me > 0
+
+    @pl.when(has_right)
+    def _():
+        greet(me + 1, ob)
+
+    @pl.when(has_left)
+    def _():
+        greet(me - 1, ob)
+
+    for t in range(1, plane):
+        greet(z * plane + (r + t) % plane, ob)
+
+    for q in range(1, planes):
+        @pl.when(q > z)
+        def _(q=q):
+            greet(q * plane + r, ob)
 
     loads = [
         pltpu.make_async_copy(src, dst, in_sem.at[n])
@@ -137,34 +164,17 @@
                 (dis_hbm, dis),
                 (cen_hbm, cen),
                 (ex_hbm, ex),
+                (cnt_hbm, counts),
+                (jas_hbm, jastrow),
+                (amp_hbm, log_amp),
                 (orb_hbm, orb),
                 (inv_hbm, inv),
                 (sla_hbm, sla),
-                (cnt_hbm, counts),
-                (jas_hbm, jastrow),
-                (amp_hbm, log_amp),
             )
         )
     ]
     for load in loads:
         load.start()
-    barrier = pltpu.get_barrier_semaphore()
-
-    def greet(w, o):
-        pl.semaphore_signal(barrier, inc=1, device_id=at(w, o), device_id_type=MESH)
-
-    greet(me, partner)
-    greet(me, across)
-    has_right, has_left = me < walkers - 1, me > 0
-
-    @pl.when(has_right)
-    def _():
-        greet(me + 1, ob)
-
-    @pl.when(has_left)
-    def _():
-        greet(me - 1, ob)
-
     @pl.when(me == 0)
     def _():
         rs_l[...] = jnp.zeros_like(rs_l)
@@ -175,13 +185,25 @@
         rs_r[...] = jnp.zeros_like(rs_r)
         ri_r[...] = jnp.zeros_like(ri_r)
 
-    @pl.loop(1, plane)
-    def _(t):
-        greet(z * plane + (r + t) % plane, ob)
-
-    @pl.loop(1, planes)
-    def _(t):
-        greet(((z + t) % planes) * plane + r, ob)
+    late = z >= planes // 2
+    early = jnp.logical_not(late)
+    eager = late & (r >= 2)
+    patient = jnp.logical_not(eager)
+
+    def enter():
+        neighbours = jnp.where(has_right, 1, 0) + jnp.where(has_left, 1, 0)
+        pl.semaphore_wait(barrier, 2 + (plane - 1) + z + neighbours)
+
+        @pl.loop(0, planes)
+        def _(q):
+            @pl.when(q < z)
+            def _():
+                pl.semaphore_signal(
+                    up_sem.at[z],
+                    inc=1,
+                    device_id=at(q * plane + r, ob),
+                    device_id_type=MESH,
+                )
 
     for load in loads[:6]:
         load.wait()
@@ -224,45 +246,9 @@
             pts[c, rows, :] = jnp.broadcast_to(old[c], (K, 128))
             pts[c + 3, rows, :] = jnp.broadcast_to(new[c], (K, 128))
 
-    for load in loads[9:]:
+    for load in loads[6:9]:
         load.wait()
     sub32 = iota((32, 128), 0)
-
-    @pl.loop(0, WD)
-    def _(w):
-        zero = jnp.zeros((32, 128), F32)
-        js, jd, es, ed = zero, zero, zero, zero
-
-        def pair_block(oc, nc, sj, falloff, ja, ea):
-            old_sq, new_sq = zero, zero
-            for c in range(3):
-                a = oc[c] - here[w, 2 * c + sj : 2 * c + sj + 1, :]
-                e = nc[c] - misc[w, 2 * c + sj : 2 * c + sj + 1, :]
-                old_sq = old_sq + a * a
-                new_sq = new_sq + e * e
-            od, nd = jnp.sqrt(old_sq), jnp.sqrt(new_sq)
-            term = (nd - od) / ((1.0 + falloff * nd) * (1.0 + falloff * od))
-            return ja + term, ea + lax.rsqrt(new_sq + 1.0)
-
-        for si in range(2):
-            for n in range(4):
-                on = lane == sub32 + 32 * n
-                oc, nc = [], []
-                for c in range(3):
-                    oi = here[w, 2 * c + si : 2 * c + si + 1, :]
-                    ni = misc[w, 2 * c + si : 2 * c + si + 1, :]
-                    oc.append(jnp.sum(jnp.where(on, oi, 0.0), axis=1, keepdims=True))
-                    nc.append(jnp.sum(jnp.where(on, ni, 0.0), axis=1, keepdims=True))
-                js, es = pair_block(oc, nc, si, jastrow[2], js, es)
-                if si == 0:
-                    jd, ed = pair_block(oc, nc, 1, jastrow[3], jd, ed)
-        ja = jastrow[0] * js + (2.0 * jastrow[1]) * jd
-        ea = es + 2.0 * ed
-        jt = jnp.sum(jnp.sum(ja, axis=0, keepdims=True), axis=1, keepdims=True)
-        st = jnp.sum(jnp.sum(ea, axis=0, keepdims=True), axis=1, keepdims=True)
-        energy = (st - 2.0 * NEL) / (2.0 * NEL * (2 * NEL - 1))
-        misc[w, 6:7, :] = jnp.broadcast_to(energy, (1, 128))
-        misc[w, 7:8, :] = jnp.broadcast_to(jt, (1, 128))
 
     l1 = iota((1, 128), 1)
     c = [counts[n] for n in range(WD)]
@@ -271,12 +257,127 @@
         limit.append(limit[-1] + c[n])
     start = [limit[n] - c[n] for n in range(WD)]
     total = limit[-1]
-    tiles = [misc[n] for n in range(WD)]
-    weighted = jnp.zeros((1, 128), F32)
-    for n in range(WD):
-        weighted = weighted + c[n].astype(F32) * tiles[n][6:7, :]
-    own = jnp.where(l1 == 0, total.astype(F32), jnp.where(l1 == 1, weighted, 0.0))
-    row_a[...] = own
+    def columns(ref, w, si, n):
+        on = lane == sub32 + 32 * n
+        got = []
+        for c in range(3):
+            row = ref[w, 2 * c + si : 2 * c + si + 1, :]
+            got.append(jnp.sum(jnp.where(on, row, 0.0), axis=1, keepdims=True))
+        return got
+
+    def squares(column, ref, w, sj):
+        out = jnp.zeros((32, 128), F32)
+        for c in range(3):
+            d = column[c] - ref[w, 2 * c + sj : 2 * c + sj + 1, :]
+            out = out + d * d
+        return out
+
+    def whole(x):
+        return jnp.sum(jnp.sum(x, axis=0, keepdims=True), axis=1, keepdims=True)
+
+    def energies():
+        @pl.loop(0, WD, unroll=True)
+        def _(w):
+            es = jnp.zeros((32, 128), F32)
+            ed = jnp.zeros((32, 128), F32)
+            for si in range(2):
+                for n in range(4):
+                    column = columns(misc, w, si, n)
+                    es = es + lax.rsqrt(squares(column, misc, w, si) + 1.0)
+                    if si == 0:
+                        ed = ed + lax.rsqrt(squares(column, misc, w, 1) + 1.0)
+            energy = (whole(es + 2.0 * ed) - 2.0 * NEL) / (2.0 * NEL * (2 * NEL - 1))
+            misc[w, 6:7, :] = jnp.broadcast_to(energy, (1, 128))
+
+        weighted = jnp.zeros((1, 128), F32)
+        for n in range(WD):
+            weighted = weighted + c[n].astype(F32) * misc[n, 6:7, :]
+        own = jnp.where(l1 == 0, total.astype(F32), jnp.where(l1 == 1, weighted, 0.0))
+        row_a[...] = own
+
+    def jastrow_change():
+        @pl.loop(0, WD)
+        def _(w):
+            def change_of(oc, nc, sj, falloff):
+                od = jnp.sqrt(squares(oc, here, w, sj))
+                nd = jnp.sqrt(squares(nc, misc, w, sj))
+                return (nd - od) / ((1.0 + falloff * nd) * (1.0 + falloff * od))
+
+            js = jnp.zeros((32, 128), F32)
+            jd = jnp.zeros((32, 128), F32)
+            for si in range(2):
+                for n in range(4):
+                    oc, nc = columns(here, w, si, n), columns(misc, w, si, n)
+                    js = js + change_of(oc, nc, si, jastrow[2])
+                    if si == 0:
+                        jd = jd + change_of(oc, nc, 1, jastrow[3])
+            jt = whole(jastrow[0] * js + (2.0 * jastrow[1]) * jd)
+            misc[w, 7:8, :] = jnp.broadcast_to(jt, (1, 128))
+
+    def in_plane(q):
+        return pltpu.make_async_remote_copy(
+            src_ref=row_a,
+            dst_ref=tab_a.at[r],
+            send_sem=send_a.at[q],
+            recv_sem=recv_a.at[r],
+            device_id=at(z * plane + q, ob),
+            device_id_type=MESH,
+        )
+
+    def from_plane(q):
+        return pltpu.make_async_remote_copy(
+            src_ref=row_a,
+            dst_ref=tab_a.at[q],
+            send_sem=send_a.at[q],
+            recv_sem=recv_a.at[q],
+            device_id=at(z * plane + q, ob),
+            device_id_type=MESH,
+        )
+
+    def send_plane():
+        @pl.loop(1, plane)
+        def _(t):
+            in_plane((r + t) % plane).start()
+
+
+    def table(tab, rows, place, own_row):
+        before = jnp.zeros((1, 128), F32)
+        every = jnp.zeros((1, 128), F32)
+        for n in range(rows):
+            x = jnp.where(jnp.full((1, 128), place, jnp.int32) == n, own_row, tab[n])
+            before = before + jnp.where(jnp.full((1, 128), place, jnp.int32) > n, x, 0.0)
+            every = every + x
+        return before, every
+
+    def in_column(q, slot):
+        return pltpu.make_async_remote_copy(
+            src_ref=row_b,
+            dst_ref=tab_b.at[slot],
+            send_sem=send_b.at[q],
+            recv_sem=recv_b.at[slot],
+            device_id=at(q * plane + r, ob),
+            device_id_type=MESH,
+        )
+
+    def send_column():
+        @pl.loop(1, plane)
+        def _(t):
+            from_plane((r + t) % plane).wait_recv()
+
+        pre[...], row_b[...] = table(tab_a, plane, r, row_a[...])
+
+        @pl.loop(0, planes)
+        def _(q):
+            @pl.when(q < z)
+            def _():
+                in_column(q, z).start()
+
+    energies()
+
+    @pl.when(eager)
+    def _():
+        enter()
+        send_plane()
 
     @pl.loop(0, 2 * WD)
     def _(b):
@@ -300,7 +401,12 @@
             dhi[s, to, span] = high
             dlo[s, to, span] = low
 
-    loads[6].wait()
+    @pl.when(patient)
+    def _():
+        enter()
+        send_plane()
+
+    loads[9].wait()
     shift = []
     for s in range(2):
         high, low = split(orb[s])
@@ -329,7 +435,7 @@
             )
         )
 
-    loads[7].wait()
+    loads[10].wait()
     change = []
     for g in range(2):
         rows = slice(g * 128, (g + 1) * 128)
@@ -340,9 +446,6 @@
     snd_a[...] = pick(mine_mask, change[1], change[0])
     part[...] = pick(mine_mask, change[0], change[1])
 
-    neighbours = jnp.where(has_right, 1, 0) + jnp.where(has_left, 1, 0)
-    pl.semaphore_wait(barrier, 2 + (plane - 1) + (planes - 1) + neighbours)
-
     def remote(src, dst, n, w, o):
         return pltpu.make_async_remote_copy(
             src_ref=src,
@@ -354,34 +457,10 @@
         )
 
     to_partner = remote(snd_a, rcv_a, 0, me, partner)
+
     to_partner.start()
 
-    def in_plane(q):
-        return pltpu.make_async_remote_copy(
-            src_ref=row_a,
-            dst_ref=tab_a.at[r],
-            send_sem=send_a.at[q],
-            recv_sem=recv_a.at[r],
-            device_id=at(z * plane + q, ob),
-            device_id_type=MESH,
-        )
-
-    def from_plane(q):
-        return pltpu.make_async_remote_copy(
-            src_ref=row_a,
-            dst_ref=tab_a.at[q],
-            send_sem=send_a.at[q],
-            recv_sem=recv_a.at[q],
-            device_id=at(z * plane + q, ob),
-            device_id_type=MESH,
-        )
-
-    @pl.loop(1, plane)
-    def _(t):
-        in_plane((r + t) % plane).start()
-
-
-    loads[8].wait()
+    loads[11].wait()
     sla_now = []
     for g in range(2):
         rows = slice(g * 128, (g + 1) * 128)
@@ -394,6 +473,14 @@
     part[...] = part[...] + rcv_a[...]
     to_across = remote(part, rcv_b, 1, me, across)
     to_across.start()
+
+    @pl.when(late)
+    def _():
+        send_column()
+
+    jastrow_change()
+
+    tiles = [misc[n] for n in range(WD)]
 
     def copy_masks(j):
         return [flag((start[n] <= j) & (j < limit[n])) for n in range(WD)]
@@ -491,6 +578,10 @@
     swap = remote(solv.at[core], solv.at[core], 2, me, partner)
     swap.start()
 
+    @pl.when(early)
+    def _():
+        send_column()
+
     swap_in = remote(solv.at[1 - core], solv.at[1 - core], 2, me, partner)
     swap_in.wait_recv()
     for g in range(2):
@@ -513,40 +604,19 @@
     inverse_left = remote(inv_l, ri_r, 6, me - 1, ob)
     start_both(inverse_right, inverse_left)
 
-    @pl.loop(1, plane)
-    def _(t):
-        from_plane((r + t) % plane).wait_recv()
-
-    def table(tab, rows, place, own_row):
-        before = jnp.zeros((1, 128), F32)
-        every = jnp.zeros((1, 128), F32)
-        for n in range(rows):
-            x = jnp.where(jnp.full((1, 128), place, jnp.int32) == n, own_row, tab[n])
-            before = before + jnp.where(jnp.full((1, 128), place, jnp.int32) > n, x, 0.0)
-            every = every + x
-        return before, every
-
-    before_a, every_a = table(tab_a, plane, r, own)
-    row_b[...] = every_a
-
-    def in_column(q, slot):
-        return pltpu.make_async_remote_copy(
-            src_ref=row_b,
-            dst_ref=tab_b.at[slot],
-            send_sem=send_b.at[q],
-            recv_sem=recv_b.at[slot],
-            device_id=at(q * plane + r, ob),
-            device_id_type=MESH,
-        )
-
     @pl.loop(1, planes)
     def _(t):
-        in_column((z + t) % planes, z).start()
+        @pl.when(z + t < planes)
+        def _():
+            pl.semaphore_wait(up_sem.at[z + t], 1)
+            in_column(z + t, z).start()
 
     @pl.loop(1, planes)
     def _(t):
         q = (z + t) % planes
         in_column(q, q).wait_recv()
+
+    every_a, before_a = row_b[...], pre[...]
 
     before_b, every_b = table(tab_b, planes, z, every_a)
     mean = jnp.sum(jnp.where(l1 == 1, every_b, 0.0), axis=1, keepdims=True)
@@ -703,6 +773,7 @@
                 *[buf(144, 128) for _ in range(8)],
                 buf(1, 128),
                 buf(1, 128),
+                buf(1, 128),
                 buf(plane, 1, 128),
                 buf(planes, 1, 128),
                 dma((12,)),
@@ -712,6 +783,7 @@
                 dma((plane,)),
                 dma((planes,)),
                 dma((planes,)),
+                pltpu.SemaphoreType.REGULAR((planes,)),
             ],
             compiler_params=pltpu.CompilerParams(
                 collective_id=0, has_side_effects=True, vmem_limit_bytes=16 << 20

time: 28.9 us -> 26.4 us (0.913)
  Pallas kernels: 28.1 us -> 25.6 us
    pallas_call x1, Pallas kernels: 27.4 us -> 24.8 us  [body(): pl.pallas_call(lambda *refs: kernel(planes, plane, *refs), out_shape=shap...]
where the time goes in v3:
time: 26.4 us; the launch traced here: 26.2 us
  Pallas kernels  25.6 us (97%)
  between operations  0.65 us (2%)
    pallas_call x1, Pallas kernels, body(): pl.pallas_call(lambda *refs: kernel(planes, plane, *refs), out_shape=shap...  24.8 us
    pallas_call x1, Pallas kernels, body(): pl.pallas_call(finish, out_shape=(shape(256, 128), shape(256, 128), shape...  0.73 us

profile of v3, /device:TPU:1, one launch (start us, length us, event | category | flops | bytes accessed | tf_op | source)
XLA Modules:
  0.0 26.2 jit_solution(11535362042378314680)
XLA Ops:
  0.6 24.8 %generation.1.packed = f32[560,128]{1,0:T(8,128)S(1)} custom-call(s32[4]{0:T(128)} %refs_0_.1, f32[4]{0:T(128)} %refs_1_.1, f32[4]{0:T(128)} %refs_2_.1, f32[256,128]{1,0:T(8,128)} %bitcast.11, f32[256,128]{1,0:T(8,128)} %bitcast.12, f32[3,4,256]{2,1,0:T(4,128)} %bitcast.13, f32[3,4,256]{2,1,0:T(4,128)} %bitcast.14, s32[8,128]{1,0:T(8,128)} %bitcast.15, ...), custom_call_target="tpu_custom_call" | custom-call | tf_op jit(solution)/shard_map/generation/pallas_call | solution.py:741
  25.5 0.7 %finish.1 = (f32[256,128]{1,0:T(8,128)}, f32[256,128]{1,0:T(8,128)}, f32[3,4,256]{2,1,0:T(4,128)}, f32[4]{0:T(128)}, f32[4]{0:T(128)}, /*index=5*/f32[1]{0:T(128)}) custom-call(f32[560,128]{1,0:T(8,128)S(1)} %generation.1.packed), custom_call_target="tpu_custom_call" | custom-call | tf_op jit(solution)/shard_map/finish/pallas_call | solution.py:806

commit v4 on v3

--- a/solution.py
+++ b/solution.py
@@ -129,31 +129,6 @@
     def at(w, o):
         return {"walkers": w, "orb": o}
 
-    barrier = pltpu.get_barrier_semaphore()
-
-    def greet(w, o):
-        pl.semaphore_signal(barrier, inc=1, device_id=at(w, o), device_id_type=MESH)
-
-    greet(me, partner)
-    greet(me, across)
-    has_right, has_left = me < walkers - 1, me > 0
-
-    @pl.when(has_right)
-    def _():
-        greet(me + 1, ob)
-
-    @pl.when(has_left)
-    def _():
-        greet(me - 1, ob)
-
-    for t in range(1, plane):
-        greet(z * plane + (r + t) % plane, ob)
-
-    for q in range(1, planes):
-        @pl.when(q > z)
-        def _(q=q):
-            greet(q * plane + r, ob)
-
     loads = [
         pltpu.make_async_copy(src, dst, in_sem.at[n])
         for n, (src, dst) in enumerate(
@@ -175,6 +150,31 @@
     ]
     for load in loads:
         load.start()
+    barrier = pltpu.get_barrier_semaphore()
+
+    def greet(w, o):
+        pl.semaphore_signal(barrier, inc=1, device_id=at(w, o), device_id_type=MESH)
+
+    greet(me, partner)
+    greet(me, across)
+    has_right, has_left = me < walkers - 1, me > 0
+
+    @pl.when(has_right)
+    def _():
+        greet(me + 1, ob)
+
+    @pl.when(has_left)
+    def _():
+        greet(me - 1, ob)
+
+    for t in range(1, plane):
+        greet(z * plane + (r + t) % plane, ob)
+
+    for q in range(1, planes):
+        @pl.when(q > z)
+        def _(q=q):
+            greet(q * plane + r, ob)
+
     @pl.when(me == 0)
     def _():
         rs_l[...] = jnp.zeros_like(rs_l)
@@ -219,7 +219,7 @@
     lane = iota((K, 128), 1)
     diag = lane == iota((K, 128), 0)
 
-    @pl.loop(0, 2 * WD)
+    @pl.loop(0, 2 * WD, unroll=4)
     def _(b):
         w, s = b // 2, b % 2
         order = mo[pl.ds(b, 1), :].astype(F32)
@@ -379,41 +379,38 @@
         enter()
         send_plane()
 
-    @pl.loop(0, 2 * WD)
-    def _(b):
-        w, s = b // 2, b % 2
-        rows = pl.ds(pl.multiple_of(b * K, K), K)
-        old = [pts[c, rows, :] for c in range(3)]
-        new = [pts[c + 3, rows, :] for c in range(3)]
-        to = pl.ds(pl.multiple_of(w * K, K), K)
-        for n in range(8):
-            span = slice(n * 128, (n + 1) * 128)
-            rate = ex[n : n + 1, :] * (-LOG2E)
-            far = jnp.zeros((K, 128), F32)
-            near = jnp.zeros((K, 128), F32)
-            for c in range(3):
-                center = cen[c : c + 1, span]
-                a, e = old[c] - center, new[c] - center
-                far = far + a * a
-                near = near + e * e
-            differ = jnp.exp2(rate * near) - jnp.exp2(rate * far)
-            high, low = split(differ)
-            dhi[s, to, span] = high
-            dlo[s, to, span] = low
+    loads[9].wait()
+    shift = [jnp.zeros((128, 128), F32)] * 2
+    for m in range(4):
+        for b in range(2 * WD):
+            w, s = b // 2, b % 2
+            rows, to = slice(b * K, (b + 1) * K), slice(w * K, (w + 1) * K)
+            for n in (2 * m, 2 * m + 1):
+                span = slice(n * 128, (n + 1) * 128)
+                rate = ex[n : n + 1, :] * (-LOG2E)
+                far = jnp.zeros((K, 128), F32)
+                near = jnp.zeros((K, 128), F32)
+                for c3 in range(3):
+                    center = cen[c3 : c3 + 1, span]
+                    a, e = pts[c3, rows, :] - center, pts[c3 + 3, rows, :] - center
+                    far = far + a * a
+                    near = near + e * e
+                high, low = split(jnp.exp2(rate * near) - jnp.exp2(rate * far))
+                dhi[s, to, span] = high
+                dlo[s, to, span] = low
+        span = slice(m * 256, (m + 1) * 256)
+        for s in range(2):
+            high, low = split(orb[s, :, span])
+            high4 = jnp.concatenate([high] * 4, axis=0)
+            low4 = jnp.concatenate([low] * 4, axis=0)
+            a = dhi[s, :, span]
+            part_sum = product(a, high4, NT) + product(a, low4, NT)
+            shift[s] = shift[s] + (part_sum + product(dlo[s, :, span], high4, NT))
 
     @pl.when(patient)
     def _():
         enter()
         send_plane()
-
-    loads[9].wait()
-    shift = []
-    for s in range(2):
-        high, low = split(orb[s])
-        high4 = jnp.concatenate([high] * 4, axis=0)
-        low4 = jnp.concatenate([low] * 4, axis=0)
-        a = dhi[s]
-        shift.append(product(a, high4, NT) + product(a, low4, NT) + product(dlo[s], high4, NT))
 
     seg = iota((K, 128), 1) // K
 
@@ -611,10 +608,25 @@
             pl.semaphore_wait(up_sem.at[z + t], 1)
             in_column(z + t, z).start()
 
+    for copy in (
+        to_partner,
+        to_across,
+        swap,
+    ):
+        copy.wait_send()
+
+    @pl.loop(1, plane)
+    def _(t):
+        in_plane((r + t) % plane).wait_send()
+
     @pl.loop(1, planes)
     def _(t):
         q = (z + t) % planes
         in_column(q, q).wait_recv()
+
+    @pl.loop(1, planes)
+    def _(t):
+        in_column((z + t) % planes, z).wait_send()
 
     every_a, before_a = row_b[...], pre[...]
 
@@ -668,13 +680,6 @@
         out[536 + i : 537 + i, :] = logs_here[0:1, :]
         out[544 + i : 545 + i, :] = small[6:7, :]
 
-    for copy in (
-        to_partner,
-        to_across,
-        swap,
-    ):
-        copy.wait_send()
-
     @pl.when(has_right)
     def _():
         slater_right.wait_send()
@@ -684,14 +689,6 @@
     def _():
         slater_left.wait_send()
         inverse_left.wait_send()
-
-    @pl.loop(1, plane)
-    def _(t):
-        in_plane((r + t) % plane).wait_send()
-
-    @pl.loop(1, planes)
-    def _(t):
-        in_column((z + t) % planes, z).wait_send()
 
 
 def finish(packed, out_inv, out_sla, out_pos, out_log, out_en, out_mean):

time: 26.4 us -> 26.1 us (0.989)
  the two profiles are of different devices: /device:TPU:1 before, /device:TPU:385 now
where the time goes in v4:
time: 26.1 us; the launch traced here: 26 us
  Pallas kernels  25.4 us (97%)
  between operations  0.65 us (2%)
    pallas_call x1, Pallas kernels, body(): pl.pallas_call(lambda *refs: kernel(planes, plane, *refs), out_shape=shap...  24.6 us
    pallas_call x1, Pallas kernels, body(): pl.pallas_call(finish, out_shape=(shape(256, 128), shape(256, 128), shape...  0.73 us

profile of v4, /device:TPU:385, one launch (start us, length us, event | category | flops | bytes accessed | tf_op | source)
XLA Modules:
  0.0 26.0 jit_solution(9563169339312559416)
XLA Ops:
  0.6 24.6 %generation.1.packed = f32[560,128]{1,0:T(8,128)S(1)} custom-call(s32[4]{0:T(128)} %refs_0_.1, f32[4]{0:T(128)} %refs_1_.1, f32[4]{0:T(128)} %refs_2_.1, f32[256,128]{1,0:T(8,128)} %bitcast.11, f32[256,128]{1,0:T(8,128)} %bitcast.12, f32[3,4,256]{2,1,0:T(4,128)} %bitcast.13, f32[3,4,256]{2,1,0:T(4,128)} %bitcast.14, s32[8,128]{1,0:T(8,128)} %bitcast.15, ...), custom_call_target="tpu_custom_call" | custom-call | tf_op jit(solution)/shard_map/generation/pallas_call | solution.py:738
  25.3 0.7 %finish.1 = (f32[256,128]{1,0:T(8,128)}, f32[256,128]{1,0:T(8,128)}, f32[3,4,256]{2,1,0:T(4,128)}, f32[4]{0:T(128)}, f32[4]{0:T(128)}, /*index=5*/f32[1]{0:T(128)}) custom-call(f32[560,128]{1,0:T(8,128)S(1)} %generation.1.packed), custom_call_target="tpu_custom_call" | custom-call | tf_op jit(solution)/shard_map/finish/pallas_call | solution.py:803

commit v5 on v4

--- a/solution.py
+++ b/solution.py
@@ -471,7 +471,7 @@
     to_across = remote(part, rcv_b, 1, me, across)
     to_across.start()
 
-    @pl.when(late)
+    @pl.when(late & (r >= 2))
     def _():
         send_column()
 
@@ -522,6 +522,10 @@
         @pl.when(has_left)
         def _():
             to_left.start()
+
+    @pl.when(late & (r < 2))
+    def _():
+        send_column()
 
     to_across.wait_recv()
     start_both(slater_right, slater_left)

time: 26.1 us -> 26 us (level)
  the two profiles are of different devices: /device:TPU:385 before, /device:TPU:1 now
where the time goes in v5:
time: 26 us; the launch traced here: 25.8 us
  Pallas kernels  25.2 us (97%)
  between operations  0.65 us (2%)
    pallas_call x1, Pallas kernels, body(): pl.pallas_call(lambda *refs: kernel(planes, plane, *refs), out_shape=shap...  24.4 us
    pallas_call x1, Pallas kernels, body(): pl.pallas_call(finish, out_shape=(shape(256, 128), shape(256, 128), shape...  0.73 us

profile of v5, /device:TPU:1, one launch (start us, length us, event | category | flops | bytes accessed | tf_op | source)
XLA Modules:
  0.0 25.8 jit_solution(7817545954308308697)
XLA Ops:
  0.6 24.4 %generation.1.packed = f32[560,128]{1,0:T(8,128)S(1)} custom-call(s32[4]{0:T(128)} %refs_0_.1, f32[4]{0:T(128)} %refs_1_.1, f32[4]{0:T(128)} %refs_2_.1, f32[256,128]{1,0:T(8,128)} %bitcast.11, f32[256,128]{1,0:T(8,128)} %bitcast.12, f32[3,4,256]{2,1,0:T(4,128)} %bitcast.13, f32[3,4,256]{2,1,0:T(4,128)} %bitcast.14, s32[8,128]{1,0:T(8,128)} %bitcast.15, ...), custom_call_target="tpu_custom_call" | custom-call | tf_op jit(solution)/shard_map/generation/pallas_call | solution.py:742
  25.1 0.7 %finish.1 = (f32[256,128]{1,0:T(8,128)}, f32[256,128]{1,0:T(8,128)}, f32[3,4,256]{2,1,0:T(4,128)}, f32[4]{0:T(128)}, f32[4]{0:T(128)}, /*index=5*/f32[1]{0:T(128)}) custom-call(f32[560,128]{1,0:T(8,128)S(1)} %generation.1.packed), custom_call_target="tpu_custom_call" | custom-call | tf_op jit(solution)/shard_map/finish/pallas_call | solution.py:807
